TPU v7x, 32 devices: a whole 2x2x4 slice. The times are simulated.
32 devices in a mesh: seq: 8 (over z, x), mp: 4 (over y, core).
Axes of the slice: x: 2, y: 2, z: 4, core: 2. Of those that a mesh axis runs over, the one named last changes fastest.
Arguments:
- tokens: bfloat16 [256, 3584], P('mp'), may hold values from -6 to 6
- gain_attn: float32 [3584], replicated, may hold values from 0.25 to 1.75
- w_query: bfloat16 [3584, 3584], P(None, 'seq'), may hold values from -0.09375 to 0.09375
- query_bias: float32 [3584], P('seq'), may hold values from -3 to 3
- cache_keys: bfloat16 [4, 8192, 128], P(None, 'seq'), may hold values from -80 to 80
- cache_values: bfloat16 [4, 8192, 128], P(None, 'seq'), may hold values from -6 to 6
- w_out: bfloat16 [3584, 3584], P(None, 'seq'), may hold values from -0.09375 to 0.09375
- gain_ffn: float32 [3584], P('seq'), may hold values from 0.25 to 1.75
- w_gate: bfloat16 [3584, 18944], P('mp', 'seq'), may hold values from -0.09375 to 0.09375
- w_up: bfloat16 [3584, 18944], P('mp', 'seq'), may hold values from -0.09375 to 0.09375
- w_down: bfloat16 [18944, 3584], P('seq', 'mp'), may hold values from -0.0625 to 0.0625
Outputs:
- attended: bfloat16 [256, 3584], P('mp', 'seq')
- layer_out: bfloat16 [256, 3584], P('mp', 'seq')
All inputs are finite; a program needn't handle non-finite values.
Results may differ from a plain program's by a relative error of at most 0.012.
The roundings to bfloat16 on the way count: a program that leaves them out, or rounds other values in their place, can miss the bound.
Values may be sent and summed in bfloat16 or wider, within the bound.
A program may use at most 64 MiB of HBM per device.

v0:
```python
import jax
import jax.numpy as jnp
from jax import lax
from jax.sharding import PartitionSpec as P

D = 3584
HEADS = 28
KV_HEADS = 4
HEAD = 128


eps = 1e-06


def expand(per_head):
    return jnp.repeat(per_head, HEAD, axis=1)


def block_attention(queries, block_keys, block_values):
    row_count = queries.shape[0]
    group_size = HEADS // KV_HEADS
    shaped = queries.reshape(row_count, KV_HEADS, group_size * HEAD)
    maxima = []
    sums = []
    outputs = []
    for head_group in range(KV_HEADS):
        block_query = shaped[:, head_group, :].reshape(row_count * group_size, HEAD)
        scores = jnp.einsum(
            "rd,kd->rk", block_query, block_keys[head_group], preferred_element_type=jnp.float32
        ) * HEAD ** (-0.5)
        highest = jnp.max(scores, axis=1, keepdims=True)
        probs = jnp.exp(scores - highest)
        weight_sum = jnp.sum(probs, axis=1)
        weighted = jnp.dot(
            probs.astype(jnp.bfloat16), block_values[head_group], preferred_element_type=jnp.float32
        )
        maxima.append(highest.reshape(row_count, group_size))
        sums.append(weight_sum.reshape(row_count, group_size))
        outputs.append(weighted.reshape(row_count, group_size * HEAD))
    return (
        jnp.concatenate(maxima, axis=1),
        jnp.concatenate(sums, axis=1),
        jnp.concatenate(outputs, axis=1),
    )


def body(
    tokens,
    gain_attn,
    w_query,
    query_bias,
    cache_keys,
    cache_values,
    w_out,
    gain_ffn,
    w_gate,
    w_up,
    w_down,
):
    col_width = w_query.shape[1]
    offset = lax.axis_index("seq") * col_width
    hidden_in = tokens.astype(jnp.float32)
    mean_sq = jnp.mean(hidden_in * hidden_in, axis=1, keepdims=True)
    normed = (hidden_in * lax.rsqrt(mean_sq + eps) * gain_attn).astype(jnp.bfloat16)
    query_cols = (jnp.dot(normed, w_query, preferred_element_type=jnp.float32) + query_bias).astype(
        jnp.bfloat16
    )
    queries = lax.all_gather(query_cols, "seq", axis=1, tiled=True)
    maxima, sums, weighted = block_attention(queries, cache_keys, cache_values)
    global_max = lax.pmax(maxima, "seq")
    rescale = jnp.exp(maxima - global_max)
    full_sums = lax.psum(sums * rescale, "seq")
    own_weighted = lax.psum_scatter(
        weighted * expand(rescale), "seq", scatter_dimension=1, tiled=True
    )
    own_sums = lax.dynamic_slice_in_dim(expand(full_sums), offset, col_width, 1)
    attended = (own_weighted / own_sums).astype(jnp.bfloat16)
    attended_full = lax.all_gather(attended, "seq", axis=1, tiled=True)
    projected = jnp.dot(attended_full, w_out, preferred_element_type=jnp.float32)
    residual = lax.dynamic_slice_in_dim(hidden_in, offset, col_width, 1) + projected
    square_sum = lax.psum(jnp.sum(residual * residual, axis=1), "seq")
    normed_ffn = (residual * lax.rsqrt(square_sum[:, None] / D + eps) * gain_ffn).astype(
        jnp.bfloat16
    )
    token_block = lax.all_gather(normed_ffn, "seq", axis=1, tiled=True)
    feature_block = lax.all_to_all(token_block, "mp", split_axis=1, concat_axis=0, tiled=True)
    gate_part = jnp.dot(feature_block, w_gate, preferred_element_type=jnp.float32)
    up_part = jnp.dot(feature_block, w_up, preferred_element_type=jnp.float32)
    gate_proj, up_proj = lax.psum((gate_part, up_part), "mp")
    activated = (jax.nn.silu(gate_proj) * up_proj).astype(jnp.bfloat16)
    down_terms = jnp.dot(activated, w_down, preferred_element_type=jnp.float32)
    token_terms = lax.all_to_all(
        down_terms.astype(jnp.bfloat16), "mp", split_axis=0, concat_axis=1, tiled=True
    ).astype(down_terms.dtype)
    ffn_sum = lax.psum_scatter(token_terms, "seq", scatter_dimension=1, tiled=True)
    layer_out = (residual + ffn_sum).astype(jnp.bfloat16)
    return (attended, layer_out)


def solution(mesh):
    placed = (
        P("mp", None),
        P(),
        P(None, "seq"),
        P("seq"),
        P(None, "seq", None),
        P(None, "seq", None),
        P(None, "seq"),
        P("seq"),
        P("mp", "seq"),
        P("mp", "seq"),
        P("seq", "mp"),
    )
    return jax.shard_map(
        body,
        mesh=mesh,
        in_specs=placed,
        out_specs=(P("mp", "seq"), P("mp", "seq")),
        check_vma=False,
    )
```

profile of v0, /device:TPU:5, one launch (start us, length us, event | category | flops | bytes accessed | tf_op | source)
XLA Modules:
  0.0 500.5 jit_solution(9761060591386497729)
XLA Ops:
  7.2 1.4 multiply_reduce_fusion.4
  8.6 3.2 fusion.9
  11.8 26.1 %all-gather = bf16[8,448,64]{1,2,0:T(8,128)(2,1)S(1)} all-gather(bf16[1,448,64]{1,2,0:T(8,128)(2,1)S(1)} %fusion.9), channel_id=1, replica_groups=mesh['seq'=8,'mp'=4] {'seq'}, dimensions={0}, use_global_device_ids=true | all-gather | bytes 516096 | tf_op jit(solution)/shard_map/all_gather | solution.py:68
  37.9 1.1 copy.31
  39.0 2.4 reshape.77
  41.4 1.9 reshape.64
  43.3 4.5 slice_reduce_fusion.3
  47.8 1.0 reshape_squeeze.13
  48.8 1.7 reshape_squeeze.15
  50.5 3.2 multiply_reduce_fusion
  53.7 1.4 reshape_broadcast_in_dim.15
  55.1 2.7 fusion.6
  57.8 2.1 fusion.10
  59.9 1.4 multiply_reduce_fusion.2
  61.4 1.0 fusion.2
  62.4 2.1 fusion.14
  64.6 1.4 reshape_broadcast_in_dim.13
  66.1 1.4 multiply_reduce_fusion.1
  67.6 0.5 fusion.4
  68.0 2.1 fusion.12
  70.2 0.7 reshape_broadcast_in_dim.14
  71.0 1.4 multiply_reduce_fusion.3
  72.5 0.5 fusion
  73.0 2.1 fusion.16
  75.1 0.8 reshape_broadcast_in_dim.12
  75.9 1.0 reshape.68
  76.9 0.8 reshape.73
  77.6 1.7 reshape.66
  79.3 0.7 reshape.71
  80.0 1.7 reshape.67
  81.7 0.8 reshape.72
  82.5 1.7 reshape.65
  84.1 0.7 reshape.70
  84.9 0.9 pad_maximum_fusion
  85.7 29.5 %pmax.7 = f32[64,28]{1,0:T(8,128)S(1)} all-reduce(f32[64,28]{1,0:T(8,128)S(1)} %pad_maximum_fusion), channel_id=1, replica_groups=mesh['seq'=8,'mp'=4] {'seq'}, use_global_device_ids=true, to_apply=%region_5.0 | all-reduce | flops 1792 | bytes 14336 | tf_op jit(solution)/shard_map/pmax | solution.py:70
  115.2 0.9 maximum_multiply_fusion
  116.5 2.7 bitcast_multiply_fusion
  119.2 3.0 copy.40
  122.2 2.0 convert_element_type.45
  124.2 26.3 %psum.28 = f32[64,28]{1,0:T(8,128)S(1)} all-reduce(f32[64,28]{1,0:T(8,128)S(1)} %get-tuple-element.8), channel_id=1, replica_groups=mesh['seq'=8,'mp'=4] {'seq'}, use_global_device_ids=true, to_apply=%region_11.0 | all-reduce | flops 1792 | bytes 14336 | tf_op jit(solution)/shard_map/psum | solution.py:72
  150.8 1.5 copy.56
  152.3 46.3 %reduce-scatter.7.cloned.1.call-done = f32[448,64]{1,0:T(8,128)} async-done(((f32[3584,64]{1,0:T(8,128)}), f32[448,64]{1,0:T(8,128)}) %reduce-scatter.7.cloned.1.call-update) | async-done | bytes 114704
  198.6 1.0 copy.41
  199.7 1.0 divide_convert_fusion
  200.7 25.8 %all-gather.1 = bf16[8,448,64]{1,2,0:T(8,128)(2,1)S(1)} all-gather(bf16[1,448,64]{1,2,0:T(8,128)(2,1)S(1)} %bitcast.99), channel_id=1, replica_groups=mesh['seq'=8,'mp'=4] {'seq'}, dimensions={0}, use_global_device_ids=true | all-gather | bytes 516096 | tf_op jit(solution)/shard_map/all_gather | solution.py:78
  226.5 1.1 copy.36
  227.6 2.4 reshape.79
  230.1 2.2 multiply_reduce_fusion.5
  232.3 15.0 %psum.29 = f32[64]{0:T(128)S(1)} all-reduce(f32[64]{0:T(128)S(1)} %get-tuple-element.18), channel_id=1, replica_groups=mesh['seq'=8,'mp'=4] {'seq'}, use_global_device_ids=true, to_apply=%region_13.0 | all-reduce | flops 64 | bytes 512 | tf_op jit(solution)/shard_map/psum | solution.py:81
  247.4 25.3 %all-gather.2 = bf16[8,448,64]{1,2,0:T(8,128)(2,1)S(1)} all-gather(bf16[1,448,64]{1,2,0:T(8,128)(2,1)S(1)} %fusion.49), channel_id=1, replica_groups=mesh['seq'=8,'mp'=4] {'seq'}, dimensions={0}, use_global_device_ids=true | all-gather | bytes 516096 | tf_op jit(solution)/shard_map/all_gather | solution.py:85
  272.7 1.1 copy.37
  273.8 2.4 reshape.81
  276.2 1.1 copy.57
  277.3 27.2 %all_to_all.32 = bf16[64,4,896]{2,0,1:T(8,128)(2,1)S(1)} all-to-all(bf16[64,4,896]{2,0,1:T(8,128)(2,1)S(1)} %bitcast.94), channel_id=1, replica_groups=mesh['seq'=8,'mp'=4] {'mp'}, dimensions={1} | all-to-all | bytes 917504 | tf_op jit(solution)/shard_map/all_to_all | solution.py:86
  304.5 5.1 %fusion.56 = f32[256,2368]{0,1:T(8,128)} fusion(bf16[256,896]{1,0:T(8,128)(2,1)S(1)} %bitcast.90, bf16[896,2368]{0,1:T(8,128)(2,1)} %param.20), kind=kOutput, calls=%fused_computation.83 | convolution fusion | flops 1086324736 | bytes 7127040 | tf_op jit(solution)/shard_map/dot_general | solution.py:88
  309.7 3.0 fusion.55
  312.7 93.1 %all-reduce.3.cloned.1.call-done = (f32[256,2368]{0,1:T(8,128)}, f32[256,2368]{0,1:T(8,128)}) async-done(((f32[256,2368]{0,1:T(8,128)}, f32[256,2368]{0,1:T(8,128)}), (f32[256,2368]{0,1:T(8,128)}, f32[256,2368]{0,1:T(8,128)})) %all-reduce.3.cloned.1.call-update) | async-done | bytes 4849680 | tf_op jit(solution)/shard_map/psum | solution.py:89
  405.8 5.3 %convolution_convert_fusion = bf16[256,896]{1,0:T(8,128)(2,1)S(1)} fusion(bf16[2368,896]{1,0:T(8,128)(2,1)} %param.21, f32[256,2368]{0,1:T(8,128)} %get-tuple-element.6, f32[256,2368]{0,1:T(8,128)} %get-tuple-element.7), kind=kOutput, calls=%fused_computation.17 | convolution fusion | flops 1090191360 | bytes 9551872 | tf_op jit(solution)/shard_map/dot_general | solution.py:91
  411.1 10.0 %all_to_all.33 = bf16[4,64,896]{2,1,0:T(8,128)(2,1)S(1)} all-to-all(bf16[4,64,896]{2,1,0:T(8,128)(2,1)S(1)} %bitcast.98), channel_id=1, replica_groups=mesh['seq'=8,'mp'=4] {'mp'}, dimensions={0} | all-to-all | bytes 917504 | tf_op jit(solution)/shard_map/all_to_all | solution.py:92
  421.1 1.0 convert_bitcast_fusion
  422.1 3.0 copy.44
  425.1 67.2 %reduce-scatter.9.cloned.1.call-done = f32[448,64]{1,0:T(8,128)} async-done(((f32[3584,64]{1,0:T(8,128)}), f32[448,64]{1,0:T(8,128)}) %reduce-scatter.9.cloned.1.call-update) | async-done | bytes 114704
  492.3 1.0 copy.43
  493.3 0.7 add_convert_fusion
  (38 shorter events, 1.3 us)
Async XLA Ops:
  7.2 222.9 %copy-start = (bf16[3584,448]{0,1:T(8,128)(2,1)S(1)}, bf16[3584,448]{0,1:T(8,128)(2,1)}, u32[]{:S(2)}) copy-start(bf16[3584,448]{0,1:T(8,128)(2,1)} %param.17) | copy-start | bytes 9633796
  7.2 191.5 %reduce-scatter.7.cloned.1.call-start = ((), (), s32[]{:S(2)}) async-start(), calls=%async_computation.4 | async-start | bytes 2064384
  55.1 2.7 copy-start.1
  55.1 2.7 copy-start.5
  61.4 1.0 copy-start.6
  72.9 3.9 copy-start.7
  72.9 6.3 %copy-start.8 = (f32[448]{0:T(512)S(1)}, f32[448]{0:T(512)}, u32[]{:S(2)}) copy-start(f32[448]{0:T(512)} %fusion.2) | copy-start | bytes 5380
  73.0 11.9 %copy-start.3 = (f32[64,7]{1,0:T(8,128)S(1)}, f32[64,7]{1,0:T(8,128)}, u32[]{:S(2)}) copy-start(f32[64,7]{1,0:T(8,128)} %reshape_broadcast_in_dim.15) | copy-start | bytes 5380
  73.0 11.9 %copy-start.4 = (f32[64,7]{1,0:T(8,128)S(1)}, f32[64,7]{1,0:T(8,128)}, u32[]{:S(2)}) copy-start(f32[64,7]{1,0:T(8,128)} %reshape_broadcast_in_dim.13) | copy-start | bytes 5380
  122.2 283.6 %all-reduce.3.cloned.1.call-start = ((), (), s32[]{:S(2)}) async-start(), calls=%async_computation.6 | async-start | bytes 9699328 | tf_op jit(solution)/shard_map/psum | solution.py:89
  200.7 31.5 %copy-start.2 = (bf16[64,448]{1,0:T(8,128)(2,1)}, bf16[64,448]{1,0:T(8,128)(2,1)S(1)}, u32[]{:S(2)}) copy-start(bf16[64,448]{1,0:T(8,128)(2,1)S(1)} %divide_convert_fusion) | copy-start | bytes 172036
  230.0 17.3 %copy-start.9 = (f32[448]{0:T(512)S(1)}, f32[448]{0:T(512)}, u32[]{:S(2)}) copy-start(f32[448]{0:T(512)} %param.18) | copy-start | bytes 5380
  277.3 32.4 %slice-start = ((s8[4243456]{0:T(1024)(128)(4,1)}), s8[4194304]{0:T(1024)(128)(4,1)S(1)}, s32[]{:S(2)}) async-start(s8[4243456]{0:T(1024)(128)(4,1)} %bitcast.88), calls=%async_computation.7 | async-start | bytes 8388608
  304.5 5.1 %slice-start.1 = ((s8[4243456]{0:T(1024)(128)(4,1)}), s8[49152]{0:T(1024)(128)(4,1)S(1)}, s32[]{:S(2)}) async-start(s8[4243456]{0:T(1024)(128)(4,1)} %bitcast.88), calls=%async_computation.8 | async-start | bytes 98304
  312.7 179.6 %reduce-scatter.9.cloned.1.call-start = ((), (), s32[]{:S(2)}) async-start(), calls=%async_computation.5 | async-start | bytes 2064384
Sparse Core Ops, SparseCore 0:
  122.3 76.3 reduce-scatter.6
  312.8 92.9 all-reduce.2
  425.2 67.0 reduce-scatter.8
where the time goes:
time: 505 us; the launch traced here: 500 us
  waiting for transfers between devices  207 us (41%)
  blocking collectives  185 us (37%)
  local copies, waits for them, and re-layouts  44.5 us (9%)
  matrix products  34.8 us (7%)
  other arithmetic  15.2 us (3%)
  between operations  14 us (3%)
    unnamed x5, waiting for transfers between devices  114 us
    psum x1, waiting for transfers between devices, body(): gate_proj, up_proj = lax.psum((gate_part, up_part), 'mp')  93.1 us
    pmax x1, blocking collectives, body(): global_max = lax.pmax(maxima, 'seq')  29.5 us
    all_to_all x1, blocking collectives, body(): lax.all_to_all(token_block, 'mp', split_axis=1, concat_axis=0, tiled=True)  27.2 us
    psum x1, blocking collectives, body(): full_sums = lax.psum(sums * rescale, 'seq')  26.3 us
    all_gather x1, blocking collectives, body(): queries = lax.all_gather(query_cols, 'seq', axis=1, tiled=True)  26.1 us
    all_gather x1, blocking collectives, body(): attended_full = lax.all_gather(attended, 'seq', axis=1, tiled=True)  25.8 us
    all_gather x1, blocking collectives, body(): token_block = lax.all_gather(normed_ffn, 'seq', axis=1, tiled=True)  25.3 us
  transfers between devices with their start and end apart: 3, of which 3 were waited for; matrix products, arithmetic and copies ran while one was open for 1% of the time, Pallas kernels for 0%

commit v1 on v0

v1 whole, which is shorter than its diff:
```python
import functools

import jax
import jax.numpy as jnp
from jax import lax
from jax.experimental import pallas as pl
from jax.experimental.pallas import tpu as pltpu
from jax.sharding import PartitionSpec as P

D = 3584
HEADS = 28
KV_HEADS = 4
HEAD = 128
GROUP = HEADS // KV_HEADS
SUM_LANE = 64

eps = 1e-06
MESH = pl.DeviceIdType.MESH
VMEM = pltpu.VMEM


class SeqPlan:
    def __init__(self, n_seq, n_mp):
        self.count = n_seq

    def dest(self, s, m, i):
        to = lax.rem(s + i, self.count)
        return to, m, to

    def my_slot(self, s, m):
        return s

    def source(self, s, m, i):
        return i, m


class MpPlan:
    def __init__(self, n_seq, n_mp):
        self.count = n_mp

    def dest(self, s, m, i):
        to = lax.rem(m + i, self.count)
        return s, to, to

    def my_slot(self, s, m):
        return m

    def source(self, s, m, i):
        return s, i


class RowsPlan:
    def __init__(self, n_seq, n_mp):
        self.count, self.per = n_seq, n_seq // n_mp

    def dest(self, s, m, i):
        to = lax.rem(s + i, self.count)
        return to, s // self.per, to

    def my_slot(self, s, m):
        return m * self.per + lax.rem(s, self.per)

    def source(self, s, m, i):
        return m * self.per + i % self.per, i // self.per


class HomePlan:
    def __init__(self, n_seq, n_mp):
        self.count, self.per, self.n_mp = n_seq, n_seq // n_mp, n_mp

    def dest(self, s, m, i):
        to_m = lax.rem(m + i // self.per, self.n_mp)
        j = lax.rem(s + i, self.per)
        return m * self.per + j, to_m, to_m * self.per + j

    def my_slot(self, s, m):
        return s

    def source(self, s, m, i):
        return i, s // self.per


def exchange_kernel(plans, spread, *refs):
    k = len(plans)
    ins, outs, sems = refs[:k], refs[k : 2 * k], refs[2 * k :]
    s, m = lax.axis_index("seq"), lax.axis_index("mp")
    barrier = pltpu.get_barrier_semaphore()
    seen = []
    for plan in plans:
        if type(plan) in seen:
            continue
        seen.append(type(plan))
        for i in range(plan.count):
            fs, fm = plan.source(s, m, i)
            pl.semaphore_signal(barrier, inc=1, device_id=(fs, fm), device_id_type=MESH)
    done = []
    total = 0
    for plan in plans:
        if type(plan) not in done:
            done.append(type(plan))
            total += plan.count
    pl.semaphore_wait(barrier, total)
    steps = max(plan.count for plan in plans)
    waits = []
    for i in range(steps):
        for a in range(k):
            plan, src, dst = plans[a], ins[a], outs[a]
            if i >= plan.count:
                continue
            send, recv = sems[2 * a], sems[2 * a + 1]
            to_s, to_m, index = plan.dest(s, m, i)
            mine = plan.my_slot(s, m)
            block = src.at[index] if spread[a] else src
            here = jnp.logical_and(to_s == s, to_m == m)
            remote = pltpu.make_async_remote_copy(
                src_ref=block,
                dst_ref=dst.at[mine],
                send_sem=send.at[i],
                recv_sem=recv.at[mine],
                device_id=(to_s, to_m),
                device_id_type=MESH,
            )
            local = pltpu.make_async_copy(block, dst.at[mine], send.at[i])

            @pl.when(here)
            def _():
                local.start()

            @pl.when(jnp.logical_not(here))
            def _():
                remote.start()

            waits.append((here, local, remote))
    for a in range(k):
        plan, src, dst = plans[a], ins[a], outs[a]
        recv = sems[2 * a + 1]
        for i in range(plan.count):
            from_s, from_m = plan.source(s, m, i)
            here = jnp.logical_and(from_s == s, from_m == m)
            block = src.at[0] if spread[a] else src

            @pl.when(jnp.logical_not(here))
            def _():
                pltpu.make_async_remote_copy(
                    src_ref=block,
                    dst_ref=dst.at[i],
                    send_sem=recv.at[i],
                    recv_sem=recv.at[i],
                    device_id=(from_s, from_m),
                    device_id_type=MESH,
                ).wait_recv()

    for here, local, remote in waits:

        @pl.when(here)
        def _():
            local.wait()

        @pl.when(jnp.logical_not(here))
        def _():
            remote.wait_send()


def exchange(name, cid, *items):
    plans = [item[0] for item in items]
    arrays = [item[1] for item in items]
    spread = [item[2] for item in items]
    shapes = []
    sems = []
    for plan, array, one_each in items:
        block = array.shape[1:] if one_each else array.shape
        shapes.append(jax.ShapeDtypeStruct((plan.count,) + block, array.dtype))
        sems += [pltpu.SemaphoreType.DMA((plan.count,))] * 2
    return pl.pallas_call(
        functools.partial(exchange_kernel, plans, spread),
        out_shape=tuple(shapes),
        in_specs=[pl.BlockSpec(memory_space=VMEM)] * len(items),
        out_specs=tuple([pl.BlockSpec(memory_space=VMEM)] * len(items)),
        scratch_shapes=sems,
        compiler_params=pltpu.CompilerParams(collective_id=cid, has_side_effects=True),
        name=name,
    )(*arrays)


def attention_kernel(q_ref, k_ref, v_ref, out_ref, stat_ref):
    rows = q_ref.shape[0]
    q = q_ref[...]
    stacked = jnp.concatenate([q[:, h * HEAD : (h + 1) * HEAD] for h in range(GROUP)], axis=0)
    scores = lax.dot_general(
        stacked, k_ref[0], (((1,), (1,)), ((), ())), preferred_element_type=jnp.float32
    ) * HEAD ** (-0.5)
    highest = jnp.max(scores, axis=1, keepdims=True)
    probs = jnp.exp(scores - highest)
    sums = jnp.sum(probs, axis=1, keepdims=True)
    weighted = jnp.dot(probs.astype(jnp.bfloat16), v_ref[0], preferred_element_type=jnp.float32)
    lane = lax.broadcasted_iota(jnp.int32, (rows, 128), 1)
    base = pl.program_id(0) * GROUP
    stats = jnp.where(base == 0, jnp.zeros((rows, 128), jnp.float32), stat_ref[...])
    for h in range(GROUP):
        part = slice(h * rows, (h + 1) * rows)
        out_ref[:, h * HEAD : (h + 1) * HEAD] = weighted[part].astype(jnp.bfloat16)
        stats = jnp.where(lane == base + h, highest[part], stats)
        stats = jnp.where(lane == base + h + SUM_LANE, sums[part], stats)
    stat_ref[...] = stats


def attention(queries, keys, values):
    rows = queries.shape[0]
    context = keys.shape[1]
    width = GROUP * HEAD
    return pl.pallas_call(
        attention_kernel,
        grid=(KV_HEADS,),
        out_shape=(
            jax.ShapeDtypeStruct((rows, D), jnp.bfloat16),
            jax.ShapeDtypeStruct((rows, 128), jnp.float32),
        ),
        in_specs=[
            pl.BlockSpec((rows, width), lambda g: (0, g)),
            pl.BlockSpec((1, context, HEAD), lambda g: (g, 0, 0)),
            pl.BlockSpec((1, context, HEAD), lambda g: (g, 0, 0)),
        ],
        out_specs=(
            pl.BlockSpec((rows, width), lambda g: (0, g)),
            pl.BlockSpec((rows, 128), lambda g: (0, 0)),
        ),
        name="block_attention",
    )(queries, keys, values)


def joined(blocks):
    count, rows, width = blocks.shape
    return blocks.transpose(1, 0, 2).reshape(rows, count * width)


def body(
    n_seq,
    n_mp,
    tokens,
    gain_attn,
    w_query,
    query_bias,
    cache_keys,
    cache_values,
    w_out,
    gain_ffn,
    w_gate,
    w_up,
    w_down,
):
    seq, mp, to_rows, home = (kind(n_seq, n_mp) for kind in (SeqPlan, MpPlan, RowsPlan, HomePlan))
    per = n_seq // n_mp
    rows = tokens.shape[0]
    col_width = w_query.shape[1]
    offset = lax.axis_index("seq") * col_width
    hidden_in = tokens.astype(jnp.float32)
    mean_sq = jnp.mean(hidden_in * hidden_in, axis=1, keepdims=True)
    normed = (hidden_in * lax.rsqrt(mean_sq + eps) * gain_attn).astype(jnp.bfloat16)
    query_cols = (jnp.dot(normed, w_query, preferred_element_type=jnp.float32) + query_bias).astype(
        jnp.bfloat16
    )
    (query_blocks,) = exchange("queries", 1, (seq, query_cols, False))
    weighted, stats = attention(joined(query_blocks), cache_keys, cache_values)
    weighted = weighted.reshape(rows, n_seq, col_width).transpose(1, 0, 2)
    weighted, stats = exchange("merge", 2, (seq, weighted, True), (seq, stats, False))
    maxima, sums = stats[:, :, :HEADS], stats[:, :, SUM_LANE : SUM_LANE + HEADS]
    rescale = jnp.exp(maxima - jnp.max(maxima, axis=0, keepdims=True))
    totals = jnp.sum(sums * rescale, axis=0, keepdims=True)
    head_of = (offset + lax.broadcasted_iota(jnp.int32, (HEADS, col_width), 1)) // HEAD
    pick = (head_of == lax.broadcasted_iota(jnp.int32, (HEADS, col_width), 0)).astype(jnp.float32)
    factor = jnp.einsum(
        "jrh,hc->jrc", rescale / totals, pick, precision=lax.Precision.HIGHEST
    )
    attended = jnp.sum(weighted.astype(jnp.float32) * factor, axis=0).astype(jnp.bfloat16)
    (attended_blocks,) = exchange("attended", 3, (seq, attended, False))
    projected = jnp.dot(joined(attended_blocks), w_out, preferred_element_type=jnp.float32)
    residual = lax.dynamic_slice_in_dim(hidden_in, offset, col_width, 1) + projected
    square_part = jnp.sum(residual * residual, axis=1)[None, :]
    scaled = (residual * gain_ffn).astype(jnp.bfloat16)
    feature_blocks, square_parts = exchange(
        "residual", 4, (to_rows, scaled, False), (seq, square_part, False)
    )
    feature_block = (
        feature_blocks.reshape(n_mp, per, rows, col_width)
        .transpose(0, 2, 1, 3)
        .reshape(n_mp * rows, per * col_width)
    )
    gate_part = jnp.dot(feature_block, w_gate, preferred_element_type=jnp.float32)
    up_part = jnp.dot(feature_block, w_up, preferred_element_type=jnp.float32)
    hidden = w_gate.shape[1]
    gate_parts, up_parts = exchange(
        "gate_up",
        5,
        (mp, gate_part.astype(jnp.bfloat16).reshape(n_mp, rows, hidden), True),
        (mp, up_part.astype(jnp.bfloat16).reshape(n_mp, rows, hidden), True),
    )
    inverse = lax.rsqrt(jnp.sum(square_parts, axis=0)[0][:, None] / D + eps)
    gate_proj = jnp.sum(gate_parts.astype(jnp.float32), axis=0) * inverse
    up_proj = jnp.sum(up_parts.astype(jnp.float32), axis=0) * inverse
    own_activated = (jax.nn.silu(gate_proj) * up_proj).astype(jnp.bfloat16)
    (activated,) = exchange("activated", 6, (mp, own_activated, False))
    activated = activated.reshape(n_mp * rows, hidden)
    down_terms = jnp.dot(activated, w_down, preferred_element_type=jnp.float32).astype(jnp.bfloat16)
    down_blocks = (
        down_terms.reshape(n_mp, rows, per, col_width)
        .transpose(0, 2, 1, 3)
        .reshape(n_mp * per, rows, col_width)
    )
    (terms,) = exchange("down", 7, (home, down_blocks, True))
    layer_out = (residual + jnp.sum(terms.astype(jnp.float32), axis=0)).astype(jnp.bfloat16)
    return (attended, layer_out)


def solution(mesh):
    placed = (
        P("mp", None),
        P(),
        P(None, "seq"),
        P("seq"),
        P(None, "seq", None),
        P(None, "seq", None),
        P(None, "seq"),
        P("seq"),
        P("mp", "seq"),
        P("mp", "seq"),
        P("seq", "mp"),
    )
    return jax.shard_map(
        functools.partial(body, mesh.shape["seq"], mesh.shape["mp"]),
        mesh=mesh,
        in_specs=placed,
        out_specs=(P("mp", "seq"), P("mp", "seq")),
        check_vma=False,
    )
```

time: 505 us -> 225 us (0.45)
  waiting for transfers between devices: 207 us -> 0 us
  blocking collectives: 185 us -> 0 us
  Pallas kernels: 0 us -> 160 us
  local copies, waits for them, and re-layouts: 44.5 us -> 27.1 us
  between operations: 14 us -> 0.78 us
  matrix products: 34.8 us -> 24.1 us
    pallas_call x0 -> x8, Pallas kernels: none -> 160 us  [the longest x7 153 us: exchange(): pl.pallas_call(functools.partial(exchange_kernel, plans, spread), out_sha...]
    unnamed x5 -> x0, waiting for transfers between devices: 114 us -> none
    psum x1 -> x0, waiting for transfers between devices: 93.1 us -> none  [body(): gate_proj, up_proj = lax.psum((gate_part, up_part), 'mp')]
    all_gather x3 -> x0, blocking collectives: 77.2 us -> none  [the longest x1 26.1 us: body(): queries = lax.all_gather(query_cols, 'seq', axis=1, tiled=True)]
    psum x2 -> x0, blocking collectives: 41.3 us -> none  [the longest x1 26.3 us: body(): full_sums = lax.psum(sums * rescale, 'seq')]
    all_to_all x2 -> x0, blocking collectives: 37.3 us -> none  [the longest x1 27.2 us: body(): lax.all_to_all(token_block, 'mp', split_axis=1, concat_axis=0, tiled=True)]
    pmax x1 -> x0, blocking collectives: 29.5 us -> none  [body(): global_max = lax.pmax(maxima, 'seq')]
    unnamed x32 -> x4, local copies, waits for them, and re-layouts: 16.9 us -> 0.02 us
  transfers between devices with their start and end apart: 3 -> 0, of which waited for: 3 -> 0; matrix products, arithmetic and copies ran while one was open for 1% -> 0% of each run, Pallas kernels for 0% -> 0%
where the time goes in v1:
time: 225 us; the launch traced here: 223 us
  Pallas kernels  160 us (71%)
  local copies, waits for them, and re-layouts  27.1 us (12%)
  matrix products  24.1 us (11%)
  other arithmetic  11.2 us (5%)
    pallas_call x7, Pallas kernels, exchange(): pl.pallas_call(functools.partial(exchange_kernel, plans, spread), out_sha...  153 us
    pallas_call x1, Pallas kernels, attention(): pl.pallas_call(attention_kernel, grid=(KV_HEADS,), out_shape=(jax.ShapeDt...  7.44 us
    dot_general x1, matrix products, body(): jnp.dot(activated, w_down, preferred_element_type=jnp.float32)  4.87 us
    reshape x2, local copies, waits for them, and re-layouts, joined(): return blocks.transpose(1, 0, 2).reshape(rows, count * width)  4.85 us
    dot_general x1, matrix products, body(): jnp.dot(feature_block, w_gate, preferred_element_type=jnp.float32)  4.85 us
    dot_general x1, matrix products, body(): up_part = jnp.dot(feature_block, w_up, preferred_element_type=jnp.float32)  4.85 us

profile of v1, /device:TPU:5, one launch (start us, length us, event | category | flops | bytes accessed | tf_op | source)
XLA Modules:
  0.0 223.3 jit_solution(3522672686019065676)
XLA Ops:
  0.6 0.0 copy-start
  0.7 1.4 multiply_reduce_fusion
  2.1 3.8 %fusion.1.refs_0_ = bf16[64,448]{1,0:T(8,128)(2,1)} fusion(bf16[3584,448]{0,1:T(8,128)(2,1)} %param.13, f32[3584]{0:T(1024)} %param.12, f32[64]{0:T(128)S(1)} %add_rsqrt_fusion.1, bf16[64,3584]{1,0:T(8,128)(2,1)} %param.11, f32[448]{0:T(512)} %param.14), kind=kOutput, calls=%fused_computation.9 | convolution fusion | flops 206495744 | bytes 3743744 | tf_op jit(solution)/shard_map/dot_general | solution.py:259
  5.8 14.6 %queries.1 = bf16[8,64,448]{2,1,0:T(8,128)(2,1)} custom-call(bf16[64,448]{1,0:T(8,128)(2,1)} %fusion.1.refs_0_), custom_call_target="tpu_custom_call" | custom-call | tf_op jit(solution)/shard_map/queries/pallas_call | solution.py:174
  20.5 2.1 copy.18
  22.6 2.4 %reshape.58.q_ref = bf16[64,3584]{1,0:T(8,128)(2,1)} reshape(bf16[64,8,448]{2,1,0:T(8,128)(2,1)} %copy.18) | data formatting | bytes 917504 | tf_op jit(solution)/shard_map/reshape | solution.py:233
  25.0 7.4 %block_attention.1 = (bf16[64,3584]{1,0:T(8,128)(2,1)}, f32[64,128]{1,0:T(8,128)}) custom-call(bf16[64,3584]{1,0:T(8,128)(2,1)} %reshape.58.q_ref, bf16[4,1024,128]{2,1,0:T(8,128)(2,1)} %k_ref.1, bf16[4,1024,128]{2,1,0:T(8,128)(2,1)} %v_ref.1), custom_call_target="tpu_custom_call" | custom-call | tf_op jit(solution)/shard_map/block_attention/pallas_call | solution.py:211
  32.5 2.4 %reshape.59 = bf16[64,8,448]{2,1,0:T(8,128)(2,1)} reshape(bf16[64,3584]{1,0:T(8,128)(2,1)} %get-tuple-element.10) | data formatting | bytes 917504 | tf_op jit(solution)/shard_map/reshape | solution.py:264
  34.9 2.0 copy.30
  36.9 19.2 %merge.1 = (bf16[8,64,448]{2,1,0:T(8,128)(2,1)}, f32[8,64,128]{2,1,0:T(8,128)}) custom-call(bf16[8,64,448]{2,1,0:T(8,128)(2,1)} %bitcast.30, f32[64,128]{1,0:T(8,128)} %get-tuple-element.11.refs_1_), custom_call_target="tpu_custom_call" | custom-call | tf_op jit(solution)/shard_map/merge/pallas_call | solution.py:174
  56.1 1.0 slice_reduce_fusion
  57.0 0.0 copy-start.1
  57.0 1.2 multiply_reduce_fusion.1
  58.2 2.4 %fusion.refs_0_ = bf16[64,448]{1,0:T(8,128)(2,1)} fusion(bf16[8,64,448]{2,1,0:T(8,128)(2,1)} %get-tuple-element.12, f32[8,64,128]{2,1,0:T(8,128)} %get-tuple-element.13, f32[64,28]{1,0:T(8,128)S(1)} %multiply_reduce_fusion.1, f32[64,28]{1,0:T(8,128)S(1)} %slice_reduce_fusion, s32[448]{0:T(512)S(1)} %get-tuple-element.21, s32[448]{0:T(512)S(1)} %get-tuple-element.22, ...), kind=kOutput, calls=%fused_computation.6 | convolution fusion | flops 77783552 | bytes 796608 | tf_op jit(solution)/shard_map/jrh,hc->jrc/dot_general | solution.py:271
  60.6 16.0 %attended.1 = bf16[8,64,448]{2,1,0:T(8,128)(2,1)} custom-call(bf16[64,448]{1,0:T(8,128)(2,1)} %fusion.refs_0_), custom_call_target="tpu_custom_call" | custom-call | tf_op jit(solution)/shard_map/attended/pallas_call | solution.py:174
  76.6 2.1 copy.21
  78.8 2.4 %reshape.60 = bf16[64,3584]{1,0:T(8,128)(2,1)} reshape(bf16[64,8,448]{2,1,0:T(8,128)(2,1)} %copy.21) | data formatting | bytes 917504 | tf_op jit(solution)/shard_map/reshape | solution.py:233
  81.2 1.1 convert_element_type.43
  82.3 0.0 copy-done
  82.3 0.0 copy-done.1
  82.3 3.4 %multiply_reduce_fusion.2 = (f32[64]{0:T(128)}, bf16[64,448]{1,0:T(8,128)(2,1)}, f32[64,448]{1,0:T(8,128)S(1)}) fusion(f32[448]{0:T(512)S(1)} %copy-done.1, bf16[64,3584]{1,0:T(8,128)(2,1)} %reshape.60, bf16[3584,448]{0,1:T(8,128)(2,1)S(1)} %copy-done, f32[64,3584]{1,0:T(8,128)S(1)} %convert_element_type.43, s32[]{:T(128)S(6)} %select_n.9), kind=kOutput, calls=%fused_computation.24 | convolution fusion | flops 205664192 | bytes 3958788 | tf_op jit(solution)/shard_map/dot_general | solution.py:276
  85.7 20.4 %residual.1 = (bf16[8,64,448]{2,1,0:T(8,128)(2,1)}, f32[8,1,64]{2,1,0:T(1,128)}) custom-call(bf16[64,448]{1,0:T(8,128)(2,1)} %get-tuple-element.19.refs_0_, f32[1,64]{1,0:T(1,128)} %bitcast.37), custom_call_target="tpu_custom_call" | custom-call | tf_op jit(solution)/shard_map/residual/pallas_call | solution.py:174
  106.1 2.4 %copy.29 = bf16[4,2,64,448]{3,1,2,0:T(2,128)(2,1)} copy(bf16[4,2,64,448]{3,2,1,0:T(8,128)(2,1)} %bitcast.36) | data formatting | bytes 917504 | tf_op jit(solution)/shard_map/reshape | solution.py:284
  108.4 2.2 reshape.62
  110.7 0.7 reduce_sum.77
  111.4 4.8 %convolution_convert_fusion = bf16[256,2368]{0,1:T(8,128)(2,1)} fusion(bf16[256,896]{1,0:T(8,128)(2,1)} %reshape.62, bf16[896,2368]{0,1:T(8,128)(2,1)} %param.20), kind=kOutput, calls=%fused_computation | convolution fusion | flops 1086930944 | bytes 5914624 | tf_op jit(solution)/shard_map/dot_general | solution.py:289
  116.2 2.4 %copy.24 = bf16[256,2368]{1,0:T(8,128)(2,1)} copy(bf16[256,2368]{0,1:T(8,128)(2,1)} %convolution_convert_fusion) | data formatting | bytes 2424832 | tf_op jit(solution)/shard_map/convert_element_type | solution.py:295
  118.6 4.8 %convolution_convert_fusion.1 = bf16[256,2368]{0,1:T(8,128)(2,1)} fusion(bf16[256,896]{1,0:T(8,128)(2,1)} %reshape.62, bf16[896,2368]{0,1:T(8,128)(2,1)} %param.19), kind=kOutput, calls=%fused_computation.1 | convolution fusion | flops 1086930944 | bytes 5914624 | tf_op jit(solution)/shard_map/dot_general | solution.py:288
  123.5 2.4 %copy.23 = bf16[256,2368]{1,0:T(8,128)(2,1)} copy(bf16[256,2368]{0,1:T(8,128)(2,1)} %convolution_convert_fusion.1) | data formatting | bytes 2424832 | tf_op jit(solution)/shard_map/convert_element_type | solution.py:294
  125.9 33.7 %gate_up.1 = (bf16[4,64,2368]{2,1,0:T(8,128)(2,1)}, bf16[4,64,2368]{2,1,0:T(8,128)(2,1)}) custom-call(bf16[4,64,2368]{2,1,0:T(8,128)(2,1)} %bitcast.29, bf16[4,64,2368]{2,1,0:T(8,128)(2,1)} %bitcast.28), custom_call_target="tpu_custom_call" | custom-call | tf_op jit(solution)/shard_map/gate_up/pallas_call | solution.py:174
  159.6 1.5 convert_reduce_fusion.1
  161.1 1.5 convert_reduce_fusion
  162.7 1.0 multiply_convert_fusion.1.refs_0_
  163.6 17.9 %activated.1 = bf16[4,64,2368]{2,1,0:T(8,128)(2,1)} custom-call(bf16[64,2368]{1,0:T(8,128)(2,1)} %multiply_convert_fusion.1.refs_0_), custom_call_target="tpu_custom_call" | custom-call | tf_op jit(solution)/shard_map/activated/pallas_call | solution.py:174
  181.6 4.9 %convolution_convert_fusion.2 = bf16[256,896]{1,0:T(8,128)(2,1)} fusion(bf16[256,2368]{1,0:T(8,128)(2,1)} %bitcast.35, bf16[2368,896]{1,0:T(8,128)(2,1)} %param.21), kind=kOutput, calls=%fused_computation.5 | convolution fusion | flops 1086554112 | bytes 5914624 | tf_op jit(solution)/shard_map/dot_general | solution.py:303
  186.4 2.3 %reshape.66 = bf16[4,64,2,448]{3,2,1,0:T(2,128)(2,1)} reshape(bf16[256,896]{1,0:T(8,128)(2,1)} %convolution_convert_fusion.2) | data formatting | bytes 917504 | tf_op jit(solution)/shard_map/reshape | solution.py:305
  188.7 1.9 copy.25
  190.6 30.9 %down.1 = bf16[8,64,448]{2,1,0:T(8,128)(2,1)} custom-call(bf16[8,64,448]{2,1,0:T(8,128)(2,1)} %bitcast.33), custom_call_target="tpu_custom_call" | custom-call | tf_op jit(solution)/shard_map/down/pallas_call | solution.py:174
  221.5 1.1 convert_reduce_fusion.2
  222.7 0.7 add_convert_fusion
  (4 shorter events, 0.0 us)
Async XLA Ops:
  0.6 81.6 %copy-start = (bf16[3584,448]{0,1:T(8,128)(2,1)S(1)}, bf16[3584,448]{0,1:T(8,128)(2,1)}, u32[]{:S(2)}) copy-start(bf16[3584,448]{0,1:T(8,128)(2,1)} %param.17) | copy-start | bytes 9633796
  57.0 25.2 %copy-start.1 = (f32[448]{0:T(512)S(1)}, f32[448]{0:T(512)}, u32[]{:S(2)}) copy-start(f32[448]{0:T(512)} %param.18) | copy-start | bytes 5380

commit v2 on v1

--- a/solution.py
+++ b/solution.py
@@ -13,6 +13,7 @@
 HEAD = 128
 GROUP = HEADS // KV_HEADS
 SUM_LANE = 64
+CHUNKS = 4
 
 eps = 1e-06
 MESH = pl.DeviceIdType.MESH
@@ -32,21 +33,6 @@
 
     def source(self, s, m, i):
         return i, m
-
-
-class MpPlan:
-    def __init__(self, n_seq, n_mp):
-        self.count = n_mp
-
-    def dest(self, s, m, i):
-        to = lax.rem(m + i, self.count)
-        return s, to, to
-
-    def my_slot(self, s, m):
-        return m
-
-    def source(self, s, m, i):
-        return s, i
 
 
 class RowsPlan:
@@ -80,85 +66,94 @@
         return i, s // self.per
 
 
+def greet(plans, s, m):
+    barrier = pltpu.get_barrier_semaphore()
+    total = 0
+    for plan in plans:
+        for i in range(plan.count):
+            pl.semaphore_signal(
+                barrier, inc=1, device_id=plan.source(s, m, i), device_id_type=MESH
+            )
+        total += plan.count
+    pl.semaphore_wait(barrier, total)
+
+
+def push(src, dst, send, recv, to):
+    return pltpu.make_async_remote_copy(
+        src_ref=src,
+        dst_ref=dst,
+        send_sem=send,
+        recv_sem=recv,
+        device_id=to,
+        device_id_type=MESH,
+    )
+
+
+class Flow:
+    def __init__(self, plan, src, dst, spread, send, recv, s, m):
+        self.plan, self.src, self.dst, self.spread = plan, src, dst, spread
+        self.send, self.recv, self.s, self.m = send, recv, s, m
+        self.started = []
+
+    def start(self, i):
+        to_s, to_m, index = self.plan.dest(self.s, self.m, i)
+        mine = self.plan.my_slot(self.s, self.m)
+        block = self.src.at[index] if self.spread else self.src
+        here = jnp.logical_and(to_s == self.s, to_m == self.m)
+        remote = push(block, self.dst.at[mine], self.send.at[i], self.recv.at[mine], (to_s, to_m))
+        local = pltpu.make_async_copy(block, self.dst.at[mine], self.send.at[i])
+
+        @pl.when(here)
+        def _():
+            local.start()
+
+        @pl.when(jnp.logical_not(here))
+        def _():
+            remote.start()
+
+        self.started.append((here, local, remote))
+
+    def arrive(self):
+        for i in range(self.plan.count):
+            from_s, from_m = self.plan.source(self.s, self.m, i)
+            block = self.src.at[0] if self.spread else self.src
+            copy = push(block, self.dst.at[i], self.recv.at[i], self.recv.at[i], (from_s, from_m))
+
+            @pl.when(jnp.logical_not(jnp.logical_and(from_s == self.s, from_m == self.m)))
+            def _():
+                copy.wait_recv()
+
+        for here, local, remote in self.started:
+
+            @pl.when(here)
+            def _():
+                local.wait()
+
+    def left(self):
+        for here, local, remote in self.started:
+
+            @pl.when(jnp.logical_not(here))
+            def _():
+                remote.wait_send()
+
+
 def exchange_kernel(plans, spread, *refs):
     k = len(plans)
     ins, outs, sems = refs[:k], refs[k : 2 * k], refs[2 * k :]
     s, m = lax.axis_index("seq"), lax.axis_index("mp")
-    barrier = pltpu.get_barrier_semaphore()
-    seen = []
-    for plan in plans:
-        if type(plan) in seen:
-            continue
-        seen.append(type(plan))
-        for i in range(plan.count):
-            fs, fm = plan.source(s, m, i)
-            pl.semaphore_signal(barrier, inc=1, device_id=(fs, fm), device_id_type=MESH)
-    done = []
-    total = 0
-    for plan in plans:
-        if type(plan) not in done:
-            done.append(type(plan))
-            total += plan.count
-    pl.semaphore_wait(barrier, total)
-    steps = max(plan.count for plan in plans)
-    waits = []
-    for i in range(steps):
-        for a in range(k):
-            plan, src, dst = plans[a], ins[a], outs[a]
-            if i >= plan.count:
-                continue
-            send, recv = sems[2 * a], sems[2 * a + 1]
-            to_s, to_m, index = plan.dest(s, m, i)
-            mine = plan.my_slot(s, m)
-            block = src.at[index] if spread[a] else src
-            here = jnp.logical_and(to_s == s, to_m == m)
-            remote = pltpu.make_async_remote_copy(
-                src_ref=block,
-                dst_ref=dst.at[mine],
-                send_sem=send.at[i],
-                recv_sem=recv.at[mine],
-                device_id=(to_s, to_m),
-                device_id_type=MESH,
-            )
-            local = pltpu.make_async_copy(block, dst.at[mine], send.at[i])
-
-            @pl.when(here)
-            def _():
-                local.start()
-
-            @pl.when(jnp.logical_not(here))
-            def _():
-                remote.start()
-
-            waits.append((here, local, remote))
-    for a in range(k):
-        plan, src, dst = plans[a], ins[a], outs[a]
-        recv = sems[2 * a + 1]
-        for i in range(plan.count):
-            from_s, from_m = plan.source(s, m, i)
-            here = jnp.logical_and(from_s == s, from_m == m)
-            block = src.at[0] if spread[a] else src
-
-            @pl.when(jnp.logical_not(here))
-            def _():
-                pltpu.make_async_remote_copy(
-                    src_ref=block,
-                    dst_ref=dst.at[i],
-                    send_sem=recv.at[i],
-                    recv_sem=recv.at[i],
-                    device_id=(from_s, from_m),
-                    device_id_type=MESH,
-                ).wait_recv()
-
-    for here, local, remote in waits:
-
-        @pl.when(here)
-        def _():
-            local.wait()
-
-        @pl.when(jnp.logical_not(here))
-        def _():
-            remote.wait_send()
+    greet(list({type(plan): plan for plan in plans}.values()), s, m)
+    flows = [
+        Flow(plans[a], ins[a], outs[a], spread[a], sems[2 * a], sems[2 * a + 1], s, m)
+        for a in range(k)
+    ]
+    for i in range(max(plan.count for plan in plans)):
+        for flow in flows:
+            if i < flow.plan.count:
+                flow.start(i)
+    for flow in flows:
+        flow.arrive()
+    for flow in flows:
+        flow.left()
 
 
 def exchange(name, cid, *items):
@@ -228,6 +223,200 @@
     )(queries, keys, values)
 
 
+def row_to_column(row):
+    k = row.shape[1]
+    across = lax.broadcasted_iota(jnp.int32, (k, k), 1)
+    down = lax.broadcasted_iota(jnp.int32, (k, k), 0)
+    return jnp.sum(jnp.where(across == down, row, 0.0), axis=1, keepdims=True)
+
+
+def ffn_kernel(plans, bounds, *refs):
+    seq, to_rows, home = plans
+    scaled, square, residual, gate_hbm, up_hbm, down_hbm, out = refs[:7]
+    refs = refs[7:]
+    gate_w, up_w, down_w, blocks, squares, features, acc, down_out, terms = refs[:9]
+    refs = refs[9:]
+    w_sems, sems = refs[0], refs[1:7]
+    c_sems = refs[7]
+    chunk_refs = refs[8:]
+    s, m = lax.axis_index("seq"), lax.axis_index("mp")
+    core, y = lax.rem(m, 2), m // 2
+    sibling = (s, y * 2 + (1 - core))
+    across = (s, (1 - y) * 2 + core)
+    rows, width = scaled.shape
+    per, n_mp = to_rows.per, home.n_mp
+    loads = [
+        pltpu.make_async_copy(gate_hbm, gate_w, w_sems.at[0]),
+        pltpu.make_async_copy(up_hbm, up_w, w_sems.at[1]),
+        pltpu.make_async_copy(down_hbm, down_w, w_sems.at[2]),
+    ]
+    for load in loads:
+        load.start()
+    barrier = pltpu.get_barrier_semaphore()
+    for peer in (sibling, across):
+        pl.semaphore_signal(barrier, inc=1, device_id=peer, device_id_type=MESH)
+    for plan in plans:
+        for i in range(plan.count):
+            pl.semaphore_signal(
+                barrier, inc=1, device_id=plan.source(s, m, i), device_id_type=MESH
+            )
+    pl.semaphore_wait(barrier, 2 + sum(plan.count for plan in plans))
+    main = Flow(to_rows, scaled, blocks, False, sems[0], sems[1], s, m)
+    side = Flow(seq, square, squares, False, sems[2], sems[3], s, m)
+    for i in range(to_rows.count):
+        main.start(i)
+    for i in range(seq.count):
+        side.start(i)
+    main.arrive()
+    order = (1 - core, 3 - core, core, 2 + core)
+    for p, t in enumerate(order):
+        features[p * rows : (p + 1) * rows, :] = jnp.concatenate(
+            [blocks[t * per + j] for j in range(per)], axis=1
+        )
+    loads[0].wait()
+    loads[1].wait()
+
+    chunks = []
+    for c, (first, last) in enumerate(bounds):
+        kept, s1_out, s1_in, s2_out, s2_in, act = chunk_refs[6 * c : 6 * c + 6]
+        sem = lambda k, c=c: c_sems.at[c, k]
+        chunks.append(
+            dict(
+                first=first, last=last, kept=kept, s1_out=s1_out, s1_in=s1_in,
+                s2_out=s2_out, s2_in=s2_in, act=act,
+                s1=push(s1_out, s1_in, sem(0), sem(1), sibling),
+                s2=push(s2_out, s2_in, sem(2), sem(3), across),
+                near=push(act.at[m], act.at[m], sem(4), sem(5), sibling),
+                far=push(act.at[m], act.at[m], sem(6), sem(7), across),
+                relay=push(act.at[across[1]], act.at[across[1]], sem(8), sem(9), sibling),
+            )
+        )
+
+    def multiply(ch):
+        for g, weight in enumerate((gate_w, up_w)):
+            part = jnp.dot(
+                features[...], weight[:, ch["first"] : ch["last"]],
+                preferred_element_type=jnp.float32,
+            )
+            for p in range(2):
+                ch["s1_out"][g, p] = part[p * rows : (p + 1) * rows].astype(jnp.bfloat16)
+                ch["kept"][g, p] = part[(p + 2) * rows : (p + 3) * rows]
+        ch["s1"].start()
+
+    def pair_sum(ch):
+        ch["s1"].wait_recv()
+        for g in range(2):
+            ch["s2_out"][g] = (
+                ch["kept"][g, 1 - y] + ch["s1_in"][g, 1 - y].astype(jnp.float32)
+            ).astype(jnp.bfloat16)
+        ch["s2"].start()
+
+    def activate(ch, inverse):
+        ch["s2"].wait_recv()
+        total = [
+            (
+                ch["kept"][g, y]
+                + ch["s1_in"][g, y].astype(jnp.float32)
+                + ch["s2_in"][g].astype(jnp.float32)
+            )
+            * inverse
+            for g in range(2)
+        ]
+        gate, up = total
+        ch["act"][m] = (gate / (1.0 + jnp.exp(-gate)) * up).astype(jnp.bfloat16)
+        ch["far"].start()
+        ch["near"].start()
+
+    for c, ch in enumerate(chunks):
+        multiply(ch)
+        if c >= 1:
+            pair_sum(chunks[c - 1])
+    pair_sum(chunks[-1])
+    side.arrive()
+    inverse = row_to_column(lax.rsqrt(jnp.sum(squares[...], axis=0) / D + eps))
+    for ch in chunks:
+        activate(ch, inverse)
+    loads[2].wait()
+    for c, ch in enumerate(chunks):
+        ch["far"].wait_recv()
+        ch["relay"].start()
+        ch["near"].wait_recv()
+        ch["relay"].wait_recv()
+        act = ch["act"][...].reshape(n_mp * rows, ch["last"] - ch["first"])
+        part = jnp.dot(
+            act, down_w[ch["first"] : ch["last"], :], preferred_element_type=jnp.float32
+        )
+        if c < len(chunks) - 1:
+            acc[...] = part if c == 0 else acc[...] + part
+        else:
+            total = part if c == 0 else acc[...] + part
+            for t in range(n_mp):
+                for j in range(per):
+                    down_out[t * per + j] = total[
+                        t * rows : (t + 1) * rows, j * width : (j + 1) * width
+                    ].astype(jnp.bfloat16)
+    last = Flow(home, down_out, terms, True, sems[4], sems[5], s, m)
+    for i in range(home.count):
+        last.start(i)
+    last.arrive()
+    result = residual[...]
+    for i in range(home.count):
+        result = result + terms[i].astype(jnp.float32)
+    out[...] = result.astype(jnp.bfloat16)
+    main.left()
+    side.left()
+    last.left()
+    for ch in chunks:
+        for name in ("s1", "s2", "near", "far", "relay"):
+            ch[name].wait_send()
+
+
+def ffn(plans, scaled, square, residual, w_gate, w_up, w_down):
+    seq, to_rows, home = plans
+    rows, width = scaled.shape
+    n_mp, n = home.n_mp, home.count
+    hidden = w_gate.shape[1]
+    step = max(128, -(-hidden // CHUNKS // 128) * 128)
+    bounds = [(at, min(at + step, hidden)) for at in range(0, hidden, step)]
+    bf16, f32 = jnp.bfloat16, jnp.float32
+    scratch = [
+        VMEM(w_gate.shape, bf16),
+        VMEM(w_up.shape, bf16),
+        VMEM(w_down.shape, bf16),
+        VMEM((n, rows, width), bf16),
+        VMEM((n, 1, rows), f32),
+        VMEM((n_mp * rows, w_gate.shape[0]), bf16),
+        VMEM((n_mp * rows, w_down.shape[1]), f32),
+        VMEM((n, rows, width), bf16),
+        VMEM((n, rows, width), bf16),
+        pltpu.SemaphoreType.DMA((3,)),
+    ]
+    scratch += [pltpu.SemaphoreType.DMA((n,))] * 6
+    scratch += [pltpu.SemaphoreType.DMA((len(bounds), 10))]
+    for first, last in bounds:
+        wide = last - first
+        scratch += [
+            VMEM((2, 2, rows, wide), f32),
+            VMEM((2, 2, rows, wide), bf16),
+            VMEM((2, 2, rows, wide), bf16),
+            VMEM((2, rows, wide), bf16),
+            VMEM((2, rows, wide), bf16),
+            VMEM((n_mp, rows, wide), bf16),
+        ]
+    vmem, anywhere = pl.BlockSpec(memory_space=VMEM), pl.BlockSpec(memory_space=pl.ANY)
+    return pl.pallas_call(
+        functools.partial(ffn_kernel, plans, bounds),
+        out_shape=jax.ShapeDtypeStruct((rows, width), bf16),
+        in_specs=[vmem] * 3 + [anywhere] * 3,
+        out_specs=vmem,
+        scratch_shapes=scratch,
+        compiler_params=pltpu.CompilerParams(
+            collective_id=4, has_side_effects=True, vmem_limit_bytes=60 * 2**20
+        ),
+        name="ffn",
+    )(scaled, square, residual, w_gate, w_up, w_down)
+
+
 def joined(blocks):
     count, rows, width = blocks.shape
     return blocks.transpose(1, 0, 2).reshape(rows, count * width)
@@ -248,8 +437,7 @@
     w_up,
     w_down,
 ):
-    seq, mp, to_rows, home = (kind(n_seq, n_mp) for kind in (SeqPlan, MpPlan, RowsPlan, HomePlan))
-    per = n_seq // n_mp
+    seq, to_rows, home = (kind(n_seq, n_mp) for kind in (SeqPlan, RowsPlan, HomePlan))
     rows = tokens.shape[0]
     col_width = w_query.shape[1]
     offset = lax.axis_index("seq") * col_width
@@ -277,37 +465,9 @@
     residual = lax.dynamic_slice_in_dim(hidden_in, offset, col_width, 1) + projected
     square_part = jnp.sum(residual * residual, axis=1)[None, :]
     scaled = (residual * gain_ffn).astype(jnp.bfloat16)
-    feature_blocks, square_parts = exchange(
-        "residual", 4, (to_rows, scaled, False), (seq, square_part, False)
-    )
-    feature_block = (
-        feature_blocks.reshape(n_mp, per, rows, col_width)
-        .transpose(0, 2, 1, 3)
-        .reshape(n_mp * rows, per * col_width)
-    )
-    gate_part = jnp.dot(feature_block, w_gate, preferred_element_type=jnp.float32)
-    up_part = jnp.dot(feature_block, w_up, preferred_element_type=jnp.float32)
-    hidden = w_gate.shape[1]
-    gate_parts, up_parts = exchange(
-        "gate_up",
-        5,
-        (mp, gate_part.astype(jnp.bfloat16).reshape(n_mp, rows, hidden), True),
-        (mp, up_part.astype(jnp.bfloat16).reshape(n_mp, rows, hidden), True),
-    )
-    inverse = lax.rsqrt(jnp.sum(square_parts, axis=0)[0][:, None] / D + eps)
-    gate_proj = jnp.sum(gate_parts.astype(jnp.float32), axis=0) * inverse
-    up_proj = jnp.sum(up_parts.astype(jnp.float32), axis=0) * inverse
-    own_activated = (jax.nn.silu(gate_proj) * up_proj).astype(jnp.bfloat16)
-    (activated,) = exchange("activated", 6, (mp, own_activated, False))
-    activated = activated.reshape(n_mp * rows, hidden)
-    down_terms = jnp.dot(activated, w_down, preferred_element_type=jnp.float32).astype(jnp.bfloat16)
-    down_blocks = (
-        down_terms.reshape(n_mp, rows, per, col_width)
-        .transpose(0, 2, 1, 3)
-        .reshape(n_mp * per, rows, col_width)
-    )
-    (terms,) = exchange("down", 7, (home, down_blocks, True))
-    layer_out = (residual + jnp.sum(terms.astype(jnp.float32), axis=0)).astype(jnp.bfloat16)
+    layer_out = ffn(
+        (seq, to_rows, home), scaled, square_part, residual, w_gate, w_up, w_down
+    )
     return (attended, layer_out)
 
 

time: 225 us -> 179 us (0.80)
  Pallas kernels: 160 us -> 133 us
  matrix products: 24.1 us -> 9.56 us
  other arithmetic: 11.2 us -> 4.62 us
    pallas_call x7 -> x3, Pallas kernels: 153 us -> 49.8 us  [exchange(): pl.pallas_call(functools.partial(exchange_kernel, plans, spread), out_sha...]
    pallas_call x0 -> x1, Pallas kernels: none -> 76.2 us  [ffn(): pl.pallas_call(functools.partial(ffn_kernel, plans, bounds), out_shape=ja...]
    unnamed x4 -> x7, local copies, waits for them, and re-layouts: 0.02 us -> 15.7 us
    dot_general x3 -> x0, matrix products: 14.6 us -> none  [the longest x1 4.87 us: body(): jnp.dot(activated, w_down, preferred_element_type=jnp.float32)]
    reshape x4 -> x0, local copies, waits for them, and re-layouts: 8.78 us -> none  [the longest x2 4.17 us: body(): down_terms.reshape(n_mp, rows, per, col_width).transpose(0, 2, 1, 3)]
    reduce_sum x4 -> x0, other arithmetic: 4.9 us -> none  [the longest x1 1.53 us: body(): gate_proj = jnp.sum(gate_parts.astype(jnp.float32), axis=0) * inverse]
    convert_element_type x2 -> x0, local copies, waits for them, and re-layouts: 4.8 us -> none  [the longest x1 2.4 us: body(): gate_part.astype(jnp.bfloat16).reshape(n_mp, rows, hidden)]
where the time goes in v2:
time: 179 us; the launch traced here: 178 us
  Pallas kernels  133 us (74%)
  local copies, waits for them, and re-layouts  29.2 us (16%)
  matrix products  9.56 us (5%)
  other arithmetic  4.62 us (3%)
    pallas_call x1, Pallas kernels, ffn(): pl.pallas_call(functools.partial(ffn_kernel, plans, bounds), out_shape=ja...  76.2 us
    pallas_call x3, Pallas kernels, exchange(): pl.pallas_call(functools.partial(exchange_kernel, plans, spread), out_sha...  49.8 us
    unnamed x7, local copies, waits for them, and re-layouts  15.7 us
    pallas_call x1, Pallas kernels, attention(): pl.pallas_call(attention_kernel, grid=(KV_HEADS,), out_shape=(jax.ShapeDt...  7.44 us
    reshape x2, local copies, waits for them, and re-layouts, joined(): return blocks.transpose(1, 0, 2).reshape(rows, count * width)  4.85 us
    reshape x2, local copies, waits for them, and re-layouts, body(): weighted = weighted.reshape(rows, n_seq, col_width).transpose(1, 0, 2)  4.43 us
    transpose x2, local copies, waits for them, and re-layouts, joined(): return blocks.transpose(1, 0, 2).reshape(rows, count * width)  4.25 us
    dot_general x1, matrix products, body(): jnp.dot(normed, w_query, preferred_element_type=jnp.float32) + query_bias  3.78 us

profile of v2, /device:TPU:5, one launch (start us, length us, event | category | flops | bytes accessed | tf_op | source)
XLA Modules:
  0.0 177.6 jit_solution(9234738468024245502)
XLA Ops:
  0.6 0.0 copy-start
  0.7 1.4 multiply_reduce_fusion
  2.1 3.8 %fusion.1.refs_0_ = bf16[64,448]{1,0:T(8,128)(2,1)} fusion(bf16[3584,448]{0,1:T(8,128)(2,1)} %param.13, f32[3584]{0:T(1024)} %param.12, f32[64]{0:T(128)S(1)} %add_rsqrt_fusion, bf16[64,3584]{1,0:T(8,128)(2,1)} %param.11, f32[448]{0:T(512)} %param.14), kind=kOutput, calls=%fused_computation.4 | convolution fusion | flops 206495744 | bytes 3743744 | tf_op jit(solution)/shard_map/dot_general | solution.py:447
  5.8 14.6 %queries.1 = bf16[8,64,448]{2,1,0:T(8,128)(2,1)} custom-call(bf16[64,448]{1,0:T(8,128)(2,1)} %fusion.1.refs_0_), custom_call_target="tpu_custom_call" | custom-call | tf_op jit(solution)/shard_map/queries/pallas_call | solution.py:169
  20.5 2.1 %copy.17 = bf16[64,8,448]{2,1,0:T(8,128)(2,1)} copy(bf16[64,8,448]{2,0,1:T(8,128)(2,1)} %bitcast.13) | data formatting | bytes 917504 | tf_op jit(solution)/shard_map/transpose | solution.py:422
  22.6 2.4 %reshape.26.q_ref = bf16[64,3584]{1,0:T(8,128)(2,1)} reshape(bf16[64,8,448]{2,1,0:T(8,128)(2,1)} %copy.17) | data formatting | bytes 917504 | tf_op jit(solution)/shard_map/reshape | solution.py:422
  25.0 7.4 %block_attention.1 = (bf16[64,3584]{1,0:T(8,128)(2,1)}, f32[64,128]{1,0:T(8,128)}) custom-call(bf16[64,3584]{1,0:T(8,128)(2,1)} %reshape.26.q_ref, bf16[4,1024,128]{2,1,0:T(8,128)(2,1)} %k_ref.1, bf16[4,1024,128]{2,1,0:T(8,128)(2,1)} %v_ref.1), custom_call_target="tpu_custom_call" | custom-call | tf_op jit(solution)/shard_map/block_attention/pallas_call | solution.py:206
  32.5 2.4 %reshape.27 = bf16[64,8,448]{2,1,0:T(8,128)(2,1)} reshape(bf16[64,3584]{1,0:T(8,128)(2,1)} %get-tuple-element.6) | data formatting | bytes 917504 | tf_op jit(solution)/shard_map/reshape | solution.py:452
  34.9 2.0 %copy.25 = bf16[64,8,448]{2,0,1:T(8,128)(2,1)} copy(bf16[64,8,448]{2,1,0:T(8,128)(2,1)} %reshape.27) | data formatting | bytes 917504 | tf_op jit(solution)/shard_map/reshape | solution.py:452
  36.9 19.2 %merge.1 = (bf16[8,64,448]{2,1,0:T(8,128)(2,1)}, f32[8,64,128]{2,1,0:T(8,128)}) custom-call(bf16[8,64,448]{2,1,0:T(8,128)(2,1)} %bitcast.12, f32[64,128]{1,0:T(8,128)} %get-tuple-element.7.refs_1_), custom_call_target="tpu_custom_call" | custom-call | tf_op jit(solution)/shard_map/merge/pallas_call | solution.py:169
  56.0 1.0 slice_reduce_fusion
  57.0 0.0 copy-start.1
  57.0 1.2 multiply_reduce_fusion.1
  58.2 2.4 %fusion.refs_0_ = bf16[64,448]{1,0:T(8,128)(2,1)} fusion(bf16[8,64,448]{2,1,0:T(8,128)(2,1)} %get-tuple-element.8, f32[8,64,128]{2,1,0:T(8,128)} %get-tuple-element.9, f32[64,28]{1,0:T(8,128)S(1)} %multiply_reduce_fusion.1, f32[64,28]{1,0:T(8,128)S(1)} %slice_reduce_fusion, s32[448]{0:T(512)S(1)} %get-tuple-element.13, s32[448]{0:T(512)S(1)} %get-tuple-element.14, ...), kind=kOutput, calls=%fused_computation.1 | convolution fusion | flops 77783552 | bytes 796608 | tf_op jit(solution)/shard_map/jrh,hc->jrc/dot_general | solution.py:459
  60.6 16.0 %attended.1 = bf16[8,64,448]{2,1,0:T(8,128)(2,1)} custom-call(bf16[64,448]{1,0:T(8,128)(2,1)} %fusion.refs_0_), custom_call_target="tpu_custom_call" | custom-call | tf_op jit(solution)/shard_map/attended/pallas_call | solution.py:169
  76.6 2.1 %copy.20 = bf16[64,8,448]{2,1,0:T(8,128)(2,1)} copy(bf16[64,8,448]{2,0,1:T(8,128)(2,1)} %bitcast.14) | data formatting | bytes 917504 | tf_op jit(solution)/shard_map/transpose | solution.py:422
  78.8 2.4 %reshape.28 = bf16[64,3584]{1,0:T(8,128)(2,1)} reshape(bf16[64,8,448]{2,1,0:T(8,128)(2,1)} %copy.20) | data formatting | bytes 917504 | tf_op jit(solution)/shard_map/reshape | solution.py:422
  81.2 1.1 convert_element_type.19
  82.3 0.0 copy-done
  82.3 0.0 copy-done.1
  82.3 3.4 %multiply_reduce_fusion.2 = (f32[64]{0:T(128)}, bf16[64,448]{1,0:T(8,128)(2,1)}, f32[64,448]{1,0:T(8,128)}) fusion(f32[448]{0:T(512)S(1)} %copy-done.1, bf16[64,3584]{1,0:T(8,128)(2,1)} %reshape.28, bf16[3584,448]{0,1:T(8,128)(2,1)S(1)} %copy-done, f32[64,3584]{1,0:T(8,128)S(1)} %convert_element_type.19, s32[]{:T(128)S(6)} %select_n.9), kind=kOutput, calls=%fused_computation.15 | convolution fusion | flops 205664192 | bytes 3958788 | tf_op jit(solution)/shard_map/dot_general | solution.py:464
  85.7 7.1 %copy.21.refs_3_ = bf16[896,2368]{1,0:T(8,128)(2,1)} copy(bf16[896,2368]{0,1:T(8,128)(2,1)} %param.19) | data formatting | bytes 8486912 | tf_op args[8]
  92.8 7.1 %copy.22.refs_4_ = bf16[896,2368]{1,0:T(8,128)(2,1)} copy(bf16[896,2368]{0,1:T(8,128)(2,1)} %param.20) | data formatting | bytes 8486912 | tf_op args[9]
  99.9 76.2 %ffn.1 = bf16[64,448]{1,0:T(8,128)(2,1)} custom-call(bf16[64,448]{1,0:T(8,128)(2,1)} %get-tuple-element.11.refs_0_, f32[1,64]{1,0:T(1,128)} %bitcast.15, f32[64,448]{1,0:T(8,128)} %get-tuple-element.12.refs_2_, bf16[896,2368]{1,0:T(8,128)(2,1)} %copy.21.refs_3_, bf16[896,2368]{1,0:T(8,128)(2,1)} %copy.22.refs_4_, bf16[2368,896]{1,0:T(8,128)(2,1)} %refs_5_.1), custom_call_target="tpu_custom_call" | custom-call | tf_op jit(solution)/shard_map/ffn/pallas_call | solution.py:407
  176.2 1.5 copy.27
  (3 shorter events, 0.0 us)
Async XLA Ops:
  0.6 81.6 %copy-start = (bf16[3584,448]{0,1:T(8,128)(2,1)S(1)}, bf16[3584,448]{0,1:T(8,128)(2,1)}, u32[]{:S(2)}) copy-start(bf16[3584,448]{0,1:T(8,128)(2,1)} %param.17) | copy-start | bytes 9633796
  57.0 25.2 %copy-start.1 = (f32[448]{0:T(512)S(1)}, f32[448]{0:T(512)}, u32[]{:S(2)}) copy-start(f32[448]{0:T(512)} %param.18) | copy-start | bytes 5380

commit v3 on v2

--- a/solution.py
+++ b/solution.py
@@ -12,7 +12,7 @@
 KV_HEADS = 4
 HEAD = 128
 GROUP = HEADS // KV_HEADS
-SUM_LANE = 64
+SUM_ROW = 8
 CHUNKS = 4
 
 eps = 1e-06
@@ -33,6 +33,12 @@
 
     def source(self, s, m, i):
         return i, m
+
+
+class StatPlan(SeqPlan):
+    def dest(self, s, m, i):
+        to = lax.rem(s + i, self.count)
+        return to, m, to // (self.count // KV_HEADS)
 
 
 class RowsPlan:
@@ -177,50 +183,129 @@
     )(*arrays)
 
 
+def gather_kernel(n, src, out, sems):
+    s, m = lax.axis_index("seq"), lax.axis_index("mp")
+    half = n // 2
+    hi, lo = s // 2, lax.rem(s, 2)
+    partner = (hi * 2 + 1 - lo, m)
+    barrier = pltpu.get_barrier_semaphore()
+    peers = [lax.rem(hi + d, half) * 2 + lo for d in range(half)]
+    for peer in peers[1:]:
+        pl.semaphore_signal(barrier, inc=1, device_id=(peer, m), device_id_type=MESH)
+    pl.semaphore_signal(barrier, inc=1, device_id=partner, device_id_type=MESH)
+    pl.semaphore_wait(barrier, half)
+    own = pltpu.make_async_copy(src, out.at[s], sems.at[4, 0])
+    own.start()
+    direct = [
+        push(src, out.at[s], sems.at[0, d], sems.at[1, d], (peers[d], m)) for d in range(1, half)
+    ]
+    for copy in direct:
+        copy.start()
+    handed = [push(src, out.at[s], sems.at[2, 0], sems.at[3, 0], partner)]
+    handed[0].start()
+    for d in range(1, half):
+        direct[d - 1].wait_recv()
+        at = lax.rem(hi + half - d, half) * 2 + lo
+        copy = push(out.at[at], out.at[at], sems.at[2, d], sems.at[3, d], partner)
+        copy.start()
+        handed.append(copy)
+    for copy in handed:
+        copy.wait_recv()
+    own.wait()
+    for copy in direct + handed:
+        copy.wait_send()
+
+
+def gather(name, cid, n, block):
+    vmem = pl.BlockSpec(memory_space=VMEM)
+    return pl.pallas_call(
+        functools.partial(gather_kernel, n),
+        out_shape=jax.ShapeDtypeStruct((n,) + block.shape, block.dtype),
+        in_specs=[vmem],
+        out_specs=vmem,
+        scratch_shapes=[pltpu.SemaphoreType.DMA((5, n // 2))],
+        compiler_params=pltpu.CompilerParams(collective_id=cid, has_side_effects=True),
+        name=name,
+    )(block)
+
+
 def attention_kernel(q_ref, k_ref, v_ref, out_ref, stat_ref):
-    rows = q_ref.shape[0]
-    q = q_ref[...]
+    count, rows, width = q_ref.shape
+    q = jnp.concatenate([q_ref[j] for j in range(count)], axis=1)
     stacked = jnp.concatenate([q[:, h * HEAD : (h + 1) * HEAD] for h in range(GROUP)], axis=0)
-    scores = lax.dot_general(
-        stacked, k_ref[0], (((1,), (1,)), ((), ())), preferred_element_type=jnp.float32
-    ) * HEAD ** (-0.5)
+    scores = times_transposed(stacked, k_ref[0]) * HEAD ** (-0.5)
     highest = jnp.max(scores, axis=1, keepdims=True)
     probs = jnp.exp(scores - highest)
     sums = jnp.sum(probs, axis=1, keepdims=True)
     weighted = jnp.dot(probs.astype(jnp.bfloat16), v_ref[0], preferred_element_type=jnp.float32)
-    lane = lax.broadcasted_iota(jnp.int32, (rows, 128), 1)
-    base = pl.program_id(0) * GROUP
-    stats = jnp.where(base == 0, jnp.zeros((rows, 128), jnp.float32), stat_ref[...])
+    side = jnp.concatenate([weighted[h * rows : (h + 1) * rows] for h in range(GROUP)], axis=1)
+    for j in range(count):
+        out_ref[j] = side[:, j * width : (j + 1) * width].astype(jnp.bfloat16)
+    stat_ref[...] = jnp.zeros_like(stat_ref)
     for h in range(GROUP):
         part = slice(h * rows, (h + 1) * rows)
-        out_ref[:, h * HEAD : (h + 1) * HEAD] = weighted[part].astype(jnp.bfloat16)
-        stats = jnp.where(lane == base + h, highest[part], stats)
-        stats = jnp.where(lane == base + h + SUM_LANE, sums[part], stats)
-    stat_ref[...] = stats
+        stat_ref[0, h : h + 1, :] = column_to_row(highest[part])
+        stat_ref[0, h + SUM_ROW : h + SUM_ROW + 1, :] = column_to_row(sums[part])
 
 
 def attention(queries, keys, values):
-    rows = queries.shape[0]
+    n, rows, width = queries.shape
     context = keys.shape[1]
-    width = GROUP * HEAD
+    count = n // KV_HEADS
+    blocks = pl.BlockSpec((count, rows, width), lambda g: (g, 0, 0))
+    cache = pl.BlockSpec((1, context, HEAD), lambda g: (g, 0, 0))
     return pl.pallas_call(
         attention_kernel,
         grid=(KV_HEADS,),
         out_shape=(
-            jax.ShapeDtypeStruct((rows, D), jnp.bfloat16),
-            jax.ShapeDtypeStruct((rows, 128), jnp.float32),
+            jax.ShapeDtypeStruct((n, rows, width), jnp.bfloat16),
+            jax.ShapeDtypeStruct((KV_HEADS, 2 * SUM_ROW, rows), jnp.float32),
         ),
-        in_specs=[
-            pl.BlockSpec((rows, width), lambda g: (0, g)),
-            pl.BlockSpec((1, context, HEAD), lambda g: (g, 0, 0)),
-            pl.BlockSpec((1, context, HEAD), lambda g: (g, 0, 0)),
-        ],
-        out_specs=(
-            pl.BlockSpec((rows, width), lambda g: (0, g)),
-            pl.BlockSpec((rows, 128), lambda g: (0, 0)),
-        ),
+        in_specs=[blocks, cache, cache],
+        out_specs=(blocks, pl.BlockSpec((1, 2 * SUM_ROW, rows), lambda g: (g, 0, 0))),
         name="block_attention",
     )(queries, keys, values)
+
+
+def merge_kernel(weighted_ref, stat_ref, out_ref):
+    n, rows, width = weighted_ref.shape
+    s = lax.axis_index("seq")
+    maxima, sums = stat_ref[:, :SUM_ROW, :], stat_ref[:, SUM_ROW:, :]
+    rescale = jnp.exp(maxima - jnp.max(maxima, axis=0, keepdims=True))
+    total = jnp.sum(sums * rescale, axis=0)
+    row = lax.broadcasted_iota(jnp.int32, (SUM_ROW, rows), 0)
+    inverse = 1.0 / jnp.where(row < GROUP, total, 1.0)
+    shape = (SUM_ROW, width)
+    column = s * width + lax.broadcasted_iota(jnp.int32, shape, 1)
+    head = lax.div(column, HEAD) - s // (n // KV_HEADS) * GROUP
+    pick = jnp.where(head == lax.broadcasted_iota(jnp.int32, shape, 0), 1.0, 0.0)
+    result = jnp.zeros((rows, width), jnp.float32)
+    for j in range(n):
+        factor = lax.dot_general(
+            rescale[j] * inverse,
+            pick,
+            (((0,), (0,)), ((), ())),
+            precision=lax.Precision.HIGHEST,
+            preferred_element_type=jnp.float32,
+        )
+        result = result + weighted_ref[j].astype(jnp.float32) * factor
+    out_ref[...] = result.astype(jnp.bfloat16)
+
+
+def project_kernel(blocks, w_out, own_tokens, gain, residual, scaled, square):
+    attended = jnp.concatenate([blocks[j] for j in range(blocks.shape[0])], axis=1)
+    total = own_tokens[...] + times_transposed(attended, w_out[...])
+    residual[...] = total
+    scaled[...] = (total * gain[...]).astype(jnp.bfloat16)
+    square[...] = column_to_row(jnp.sum(total * total, axis=1, keepdims=True))
+
+
+def simple(kernel, out_shape, *arrays):
+    return pl.pallas_call(kernel, out_shape=out_shape, name=kernel.__name__)(*arrays)
+
+
+def times_transposed(a, b):
+    return lax.dot_general(a, b, (((1,), (1,)), ((), ())), preferred_element_type=jnp.float32)
 
 
 def row_to_column(row):
@@ -228,6 +313,13 @@
     across = lax.broadcasted_iota(jnp.int32, (k, k), 1)
     down = lax.broadcasted_iota(jnp.int32, (k, k), 0)
     return jnp.sum(jnp.where(across == down, row, 0.0), axis=1, keepdims=True)
+
+
+def column_to_row(column):
+    k = column.shape[0]
+    across = lax.broadcasted_iota(jnp.int32, (k, k), 1)
+    down = lax.broadcasted_iota(jnp.int32, (k, k), 0)
+    return jnp.sum(jnp.where(across == down, column, 0.0), axis=0, keepdims=True)
 
 
 def ffn_kernel(plans, bounds, *refs):
@@ -294,10 +386,7 @@
 
     def multiply(ch):
         for g, weight in enumerate((gate_w, up_w)):
-            part = jnp.dot(
-                features[...], weight[:, ch["first"] : ch["last"]],
-                preferred_element_type=jnp.float32,
-            )
+            part = times_transposed(features[...], weight[ch["first"] : ch["last"], :])
             for p in range(2):
                 ch["s1_out"][g, p] = part[p * rows : (p + 1) * rows].astype(jnp.bfloat16)
                 ch["kept"][g, p] = part[(p + 2) * rows : (p + 3) * rows]
@@ -375,7 +464,7 @@
     seq, to_rows, home = plans
     rows, width = scaled.shape
     n_mp, n = home.n_mp, home.count
-    hidden = w_gate.shape[1]
+    hidden = w_gate.shape[0]
     step = max(128, -(-hidden // CHUNKS // 128) * 128)
     bounds = [(at, min(at + step, hidden)) for at in range(0, hidden, step)]
     bf16, f32 = jnp.bfloat16, jnp.float32
@@ -385,7 +474,7 @@
         VMEM(w_down.shape, bf16),
         VMEM((n, rows, width), bf16),
         VMEM((n, 1, rows), f32),
-        VMEM((n_mp * rows, w_gate.shape[0]), bf16),
+        VMEM((n_mp * rows, w_gate.shape[1]), bf16),
         VMEM((n_mp * rows, w_down.shape[1]), f32),
         VMEM((n, rows, width), bf16),
         VMEM((n, rows, width), bf16),
@@ -417,11 +506,6 @@
     )(scaled, square, residual, w_gate, w_up, w_down)
 
 
-def joined(blocks):
-    count, rows, width = blocks.shape
-    return blocks.transpose(1, 0, 2).reshape(rows, count * width)
-
-
 def body(
     n_seq,
     n_mp,
@@ -447,26 +531,25 @@
     query_cols = (jnp.dot(normed, w_query, preferred_element_type=jnp.float32) + query_bias).astype(
         jnp.bfloat16
     )
-    (query_blocks,) = exchange("queries", 1, (seq, query_cols, False))
-    weighted, stats = attention(joined(query_blocks), cache_keys, cache_values)
-    weighted = weighted.reshape(rows, n_seq, col_width).transpose(1, 0, 2)
-    weighted, stats = exchange("merge", 2, (seq, weighted, True), (seq, stats, False))
-    maxima, sums = stats[:, :, :HEADS], stats[:, :, SUM_LANE : SUM_LANE + HEADS]
-    rescale = jnp.exp(maxima - jnp.max(maxima, axis=0, keepdims=True))
-    totals = jnp.sum(sums * rescale, axis=0, keepdims=True)
-    head_of = (offset + lax.broadcasted_iota(jnp.int32, (HEADS, col_width), 1)) // HEAD
-    pick = (head_of == lax.broadcasted_iota(jnp.int32, (HEADS, col_width), 0)).astype(jnp.float32)
-    factor = jnp.einsum(
-        "jrh,hc->jrc", rescale / totals, pick, precision=lax.Precision.HIGHEST
-    )
-    attended = jnp.sum(weighted.astype(jnp.float32) * factor, axis=0).astype(jnp.bfloat16)
-    (attended_blocks,) = exchange("attended", 3, (seq, attended, False))
-    projected = jnp.dot(joined(attended_blocks), w_out, preferred_element_type=jnp.float32)
-    residual = lax.dynamic_slice_in_dim(hidden_in, offset, col_width, 1) + projected
-    square_part = jnp.sum(residual * residual, axis=1)[None, :]
-    scaled = (residual * gain_ffn).astype(jnp.bfloat16)
+    query_blocks = gather("queries", 1, n_seq, query_cols)
+    weighted, stats = attention(query_blocks, cache_keys, cache_values)
+    weighted, stats = exchange(
+        "merge", 2, (seq, weighted, True), (StatPlan(n_seq, n_mp), stats, True)
+    )
+    block = jax.ShapeDtypeStruct((rows, col_width), jnp.bfloat16)
+    wide = jax.ShapeDtypeStruct((rows, col_width), jnp.float32)
+    attended = simple(merge_kernel, block, weighted, stats)
+    attended_blocks = gather("attended", 3, n_seq, attended)
+    residual, scaled, square_part = simple(
+        project_kernel,
+        (wide, block, jax.ShapeDtypeStruct((1, rows), jnp.float32)),
+        attended_blocks,
+        w_out.T,
+        lax.dynamic_slice_in_dim(hidden_in, offset, col_width, 1),
+        gain_ffn[None, :],
+    )
     layer_out = ffn(
-        (seq, to_rows, home), scaled, square_part, residual, w_gate, w_up, w_down
+        (seq, to_rows, home), scaled, square_part, residual, w_gate.T, w_up.T, w_down
     )
     return (attended, layer_out)
 

time: 179 us -> 138 us (0.77)
  local copies, waits for them, and re-layouts: 29.2 us -> 2.89 us
  matrix products: 9.56 us -> 2.71 us
  Pallas kernels: 133 us -> 129 us
  other arithmetic: 4.62 us -> 2.45 us
    pallas_call x3 -> x1, Pallas kernels: 49.8 us -> 8.7 us  [exchange(): pl.pallas_call(functools.partial(exchange_kernel, plans, spread), out_sha...]
    pallas_call x0 -> x4, Pallas kernels: none -> 40.7 us  [the longest x2 34.2 us: gather(): pl.pallas_call(functools.partial(gather_kernel, n), out_shape=jax.ShapeDt...]
    unnamed x7 -> x3, local copies, waits for them, and re-layouts: 15.7 us -> 2.14 us
    reshape x4 -> x0, local copies, waits for them, and re-layouts: 9.28 us -> none  [the longest x2 4.85 us: joined(): return blocks.transpose(1, 0, 2).reshape(rows, count * width)]
    dot_general x2 -> x0, matrix products: 5.78 us -> none  [the longest x1 3.39 us: body(): jnp.dot(joined(attended_blocks), w_out, preferred_element_type=jnp.float32)]
    pallas_call x1, Pallas kernels: 76.2 us -> 71.8 us  [ffn(): pl.pallas_call(functools.partial(ffn_kernel, plans, bounds), out_shape=ja...]
    transpose x2 -> x0, local copies, waits for them, and re-layouts: 4.25 us -> none  [joined(): return blocks.transpose(1, 0, 2).reshape(rows, count * width)]
where the time goes in v3:
time: 138 us
  Pallas kernels  129 us (93%)
  local copies, waits for them, and re-layouts  2.89 us (2%)
  matrix products  2.71 us (2%)
  other arithmetic  2.45 us (2%)
    pallas_call x1, Pallas kernels, ffn(): pl.pallas_call(functools.partial(ffn_kernel, plans, bounds), out_shape=ja...  71.8 us
    pallas_call x2, Pallas kernels, gather(): pl.pallas_call(functools.partial(gather_kernel, n), out_shape=jax.ShapeDt...  34.2 us
    pallas_call x1, Pallas kernels, exchange(): pl.pallas_call(functools.partial(exchange_kernel, plans, spread), out_sha...  8.7 us
    pallas_call x1, Pallas kernels, attention(): pl.pallas_call(attention_kernel, grid=(KV_HEADS,), out_shape=(jax.ShapeDt...  7.88 us
    pallas_call x2, Pallas kernels, simple(): pl.pallas_call(kernel, out_shape=out_shape, name=kernel.__name__)(*arrays)  6.48 us

profile of v3, /device:TPU:5, one launch (start us, length us, event | category | flops | bytes accessed | tf_op | source)
XLA Modules:
  0.0 137.8 jit_solution(5477354122134858451)
XLA Ops:
  0.6 0.0 copy-start
  0.7 1.4 multiply_reduce_fusion
  2.0 0.7 copy-done
  2.7 2.7 %fusion.src = bf16[64,448]{1,0:T(8,128)(2,1)} fusion(bf16[3584,448]{0,1:T(8,128)(2,1)S(1)} %copy-done, f32[3584]{0:T(1024)} %param.12, f32[64]{0:T(128)S(1)} %add_rsqrt_fusion, bf16[64,3584]{1,0:T(8,128)(2,1)} %param.11, f32[448]{0:T(512)} %param.14), kind=kOutput, calls=%fused_computation.1 | convolution fusion | flops 206495744 | bytes 3743744 | tf_op jit(solution)/shard_map/dot_general | solution.py:531
  5.4 15.3 %queries.1.q_ref = bf16[8,64,448]{2,1,0:T(8,128)(2,1)} custom-call(bf16[64,448]{1,0:T(8,128)(2,1)} %fusion.src), custom_call_target="tpu_custom_call" | custom-call | tf_op jit(solution)/shard_map/queries/pallas_call | solution.py:221
  20.7 7.9 %block_attention.1 = (bf16[8,64,448]{2,1,0:T(8,128)(2,1)}, f32[4,16,64]{2,1,0:T(8,128)}) custom-call(bf16[8,64,448]{2,1,0:T(8,128)(2,1)} %queries.1.q_ref, bf16[4,1024,128]{2,1,0:T(8,128)(2,1)} %k_ref.1, bf16[4,1024,128]{2,1,0:T(8,128)(2,1)} %v_ref.1), custom_call_target="tpu_custom_call" | custom-call | tf_op jit(solution)/shard_map/block_attention/pallas_call | solution.py:257
  28.6 8.7 %merge.1 = (bf16[8,64,448]{2,1,0:T(8,128)(2,1)}, f32[8,16,64]{2,1,0:T(8,128)}) custom-call(bf16[8,64,448]{2,1,0:T(8,128)(2,1)} %get-tuple-element.9.refs_0_, f32[4,16,64]{2,1,0:T(8,128)} %get-tuple-element.10.refs_1_), custom_call_target="tpu_custom_call" | custom-call | tf_op jit(solution)/shard_map/merge/pallas_call | solution.py:175
  37.3 2.7 %merge_kernel.1.src = bf16[64,448]{1,0:T(8,128)(2,1)} custom-call(bf16[8,64,448]{2,1,0:T(8,128)(2,1)} %get-tuple-element.11.weighted_ref, f32[8,16,64]{2,1,0:T(8,128)} %get-tuple-element.12.stat_ref), custom_call_target="tpu_custom_call" | custom-call | tf_op jit(solution)/shard_map/merge_kernel/pallas_call | solution.py:304
  40.0 18.9 %attended.1.blocks = bf16[8,64,448]{2,1,0:T(8,128)(2,1)} custom-call(bf16[64,448]{1,0:T(8,128)(2,1)} %merge_kernel.1.src), custom_call_target="tpu_custom_call" | custom-call | tf_op jit(solution)/shard_map/attended/pallas_call | solution.py:221
  58.9 1.1 convert_element_type.9
  60.0 0.8 constant_dynamic-slice_fusion.own_tokens
  60.8 3.8 %project_kernel.1 = (f32[64,448]{1,0:T(8,128)}, bf16[64,448]{1,0:T(8,128)(2,1)}, f32[1,64]{1,0:T(1,128)}) custom-call(bf16[8,64,448]{2,1,0:T(8,128)(2,1)} %attended.1.blocks, bf16[448,3584]{1,0:T(8,128)(2,1)} %bitcast.7, f32[64,448]{1,0:T(8,128)} %constant_dynamic-slice_fusion.own_tokens, f32[1,448]{1,0:T(1,128)} %bitcast.8), custom_call_target="tpu_custom_call" | custom-call | tf_op jit(solution)/shard_map/project_kernel/pallas_call | solution.py:304
  64.5 71.8 %ffn.1 = bf16[64,448]{1,0:T(8,128)(2,1)} custom-call(bf16[64,448]{1,0:T(8,128)(2,1)} %get-tuple-element.13.refs_0_, f32[1,64]{1,0:T(1,128)} %get-tuple-element.14.refs_1_, f32[64,448]{1,0:T(8,128)} %get-tuple-element.15.refs_2_, bf16[2368,896]{1,0:T(8,128)(2,1)} %bitcast.5, bf16[2368,896]{1,0:T(8,128)(2,1)} %bitcast.6, bf16[2368,896]{1,0:T(8,128)(2,1)} %refs_5_.1), custom_call_target="tpu_custom_call" | custom-call | tf_op jit(solution)/shard_map/ffn/pallas_call | solution.py:496
  136.3 1.5 %copy.14 = bf16[64,448]{1,0:T(8,128)(2,1)} copy(bf16[64,448]{1,0:T(8,128)(2,1)} %ffn.1) | data formatting | bytes 114688
  (1 shorter events, 0.0 us)
Async XLA Ops:
  0.6 2.1 %copy-start = (bf16[3584,448]{0,1:T(8,128)(2,1)S(1)}, bf16[3584,448]{0,1:T(8,128)(2,1)}, u32[]{:S(2)}) copy-start(bf16[3584,448]{0,1:T(8,128)(2,1)} %param.13) | copy-start | bytes 9633796

commit v4 on v3

--- a/solution.py
+++ b/solution.py
@@ -13,7 +13,8 @@
 HEAD = 128
 GROUP = HEADS // KV_HEADS
 SUM_ROW = 8
-CHUNKS = 4
+CHUNKS = 2
+HALVES = 2
 
 eps = 1e-06
 MESH = pl.DeviceIdType.MESH
@@ -328,14 +329,14 @@
     refs = refs[7:]
     gate_w, up_w, down_w, blocks, squares, features, acc, down_out, terms = refs[:9]
     refs = refs[9:]
-    w_sems, sems = refs[0], refs[1:7]
-    c_sems = refs[7]
-    chunk_refs = refs[8:]
+    w_sems, sems = refs[0], refs[1 : 3 + 4 * HALVES]
+    c_sems = refs[3 + 4 * HALVES]
+    chunk_refs = refs[4 + 4 * HALVES :]
     s, m = lax.axis_index("seq"), lax.axis_index("mp")
     core, y = lax.rem(m, 2), m // 2
     sibling = (s, y * 2 + (1 - core))
     across = (s, (1 - y) * 2 + core)
-    rows, width = scaled.shape
+    rows, width = scaled.shape[0] // HALVES, scaled.shape[1]
     per, n_mp = to_rows.per, home.n_mp
     loads = [
         pltpu.make_async_copy(gate_hbm, gate_w, w_sems.at[0]),
@@ -353,28 +354,35 @@
                 barrier, inc=1, device_id=plan.source(s, m, i), device_id_type=MESH
             )
     pl.semaphore_wait(barrier, 2 + sum(plan.count for plan in plans))
-    main = Flow(to_rows, scaled, blocks, False, sems[0], sems[1], s, m)
-    side = Flow(seq, square, squares, False, sems[2], sems[3], s, m)
-    for i in range(to_rows.count):
-        main.start(i)
+    mains = [
+        Flow(
+            to_rows, scaled.at[pl.ds(h * rows, rows)], blocks.at[h], False,
+            sems[2 + 4 * h], sems[3 + 4 * h], s, m,
+        )
+        for h in range(HALVES)
+    ]
+    side = Flow(seq, square, squares, False, sems[0], sems[1], s, m)
+    for main in mains:
+        for i in range(to_rows.count):
+            main.start(i)
     for i in range(seq.count):
         side.start(i)
-    main.arrive()
     order = (1 - core, 3 - core, core, 2 + core)
-    for p, t in enumerate(order):
-        features[p * rows : (p + 1) * rows, :] = jnp.concatenate(
-            [blocks[t * per + j] for j in range(per)], axis=1
-        )
-    loads[0].wait()
-    loads[1].wait()
+
+    def collect(h):
+        mains[h].arrive()
+        for p, t in enumerate(order):
+            features[h, p * rows : (p + 1) * rows, :] = jnp.concatenate(
+                [blocks[h, t * per + j] for j in range(per)], axis=1
+            )
 
     chunks = []
-    for c, (first, last) in enumerate(bounds):
+    for c, (h, first, last) in enumerate(bounds):
         kept, s1_out, s1_in, s2_out, s2_in, act = chunk_refs[6 * c : 6 * c + 6]
         sem = lambda k, c=c: c_sems.at[c, k]
         chunks.append(
             dict(
-                first=first, last=last, kept=kept, s1_out=s1_out, s1_in=s1_in,
+                half=h, first=first, last=last, kept=kept, s1_out=s1_out, s1_in=s1_in,
                 s2_out=s2_out, s2_in=s2_in, act=act,
                 s1=push(s1_out, s1_in, sem(0), sem(1), sibling),
                 s2=push(s2_out, s2_in, sem(2), sem(3), across),
@@ -386,7 +394,7 @@
 
     def multiply(ch):
         for g, weight in enumerate((gate_w, up_w)):
-            part = times_transposed(features[...], weight[ch["first"] : ch["last"], :])
+            part = times_transposed(features[ch["half"]], weight[ch["first"] : ch["last"], :])
             for p in range(2):
                 ch["s1_out"][g, p] = part[p * rows : (p + 1) * rows].astype(jnp.bfloat16)
                 ch["kept"][g, p] = part[(p + 2) * rows : (p + 3) * rows]
@@ -416,45 +424,67 @@
         ch["far"].start()
         ch["near"].start()
 
-    for c, ch in enumerate(chunks):
+    def finish(h):
+        own = halves[h]
+        for c, ch in enumerate(own):
+            ch["far"].wait_recv()
+            ch["relay"].start()
+            ch["near"].wait_recv()
+            ch["relay"].wait_recv()
+            act = ch["act"][...].reshape(n_mp * rows, ch["last"] - ch["first"])
+            part = jnp.dot(
+                act, down_w[ch["first"] : ch["last"], :], preferred_element_type=jnp.float32
+            )
+            total = part if c == 0 else acc[...] + part
+            if c < len(own) - 1:
+                acc[...] = total
+        for t in range(n_mp):
+            for j in range(per):
+                down_out[h, t * per + j] = total[
+                    t * rows : (t + 1) * rows, j * width : (j + 1) * width
+                ].astype(jnp.bfloat16)
+        flow = Flow(
+            home, down_out.at[h], terms.at[h], True, sems[4 + 4 * h], sems[5 + 4 * h], s, m
+        )
+        for i in range(home.count):
+            flow.start(i)
+        return flow
+
+    halves = [[ch for ch in chunks if ch["half"] == h] for h in range(HALVES)]
+    collect(0)
+    loads[0].wait()
+    loads[1].wait()
+    for c, ch in enumerate(halves[0]):
         multiply(ch)
         if c >= 1:
-            pair_sum(chunks[c - 1])
-    pair_sum(chunks[-1])
+            pair_sum(halves[0][c - 1])
+    pair_sum(halves[0][-1])
     side.arrive()
     inverse = row_to_column(lax.rsqrt(jnp.sum(squares[...], axis=0) / D + eps))
-    for ch in chunks:
-        activate(ch, inverse)
-    loads[2].wait()
-    for c, ch in enumerate(chunks):
-        ch["far"].wait_recv()
-        ch["relay"].start()
-        ch["near"].wait_recv()
-        ch["relay"].wait_recv()
-        act = ch["act"][...].reshape(n_mp * rows, ch["last"] - ch["first"])
-        part = jnp.dot(
-            act, down_w[ch["first"] : ch["last"], :], preferred_element_type=jnp.float32
-        )
-        if c < len(chunks) - 1:
-            acc[...] = part if c == 0 else acc[...] + part
-        else:
-            total = part if c == 0 else acc[...] + part
-            for t in range(n_mp):
-                for j in range(per):
-                    down_out[t * per + j] = total[
-                        t * rows : (t + 1) * rows, j * width : (j + 1) * width
-                    ].astype(jnp.bfloat16)
-    last = Flow(home, down_out, terms, True, sems[4], sems[5], s, m)
-    for i in range(home.count):
-        last.start(i)
-    last.arrive()
-    result = residual[...]
-    for i in range(home.count):
-        result = result + terms[i].astype(jnp.float32)
-    out[...] = result.astype(jnp.bfloat16)
-    main.left()
-    side.left()
-    last.left()
+    finals = []
+    for h in range(1, HALVES):
+        collect(h)
+        for ch in halves[h]:
+            multiply(ch)
+        for ch in halves[h - 1]:
+            activate(ch, inverse[(h - 1) * rows : h * rows])
+        for ch in halves[h]:
+            pair_sum(ch)
+        if h == 1:
+            loads[2].wait()
+        finals.append(finish(h - 1))
+    for ch in halves[-1]:
+        activate(ch, inverse[(HALVES - 1) * rows : HALVES * rows])
+    finals.append(finish(HALVES - 1))
+    for h, flow in enumerate(finals):
+        flow.arrive()
+        part = slice(h * rows, (h + 1) * rows)
+        result = residual[part, :]
+        for i in range(home.count):
+            result = result + terms[h, i].astype(jnp.float32)
+        out[part, :] = result.astype(jnp.bfloat16)
+    for flow in mains + [side] + finals:
+        flow.left()
     for ch in chunks:
         for name in ("s1", "s2", "near", "far", "relay"):
             ch[name].wait_send()
@@ -466,31 +496,36 @@
     n_mp, n = home.n_mp, home.count
     hidden = w_gate.shape[0]
     step = max(128, -(-hidden // CHUNKS // 128) * 128)
-    bounds = [(at, min(at + step, hidden)) for at in range(0, hidden, step)]
+    bounds = [
+        (h, at, min(at + step, hidden))
+        for h in range(HALVES)
+        for at in range(0, hidden, step)
+    ]
+    part = rows // HALVES
     bf16, f32 = jnp.bfloat16, jnp.float32
     scratch = [
         VMEM(w_gate.shape, bf16),
         VMEM(w_up.shape, bf16),
         VMEM(w_down.shape, bf16),
-        VMEM((n, rows, width), bf16),
+        VMEM((HALVES, n, part, width), bf16),
         VMEM((n, 1, rows), f32),
-        VMEM((n_mp * rows, w_gate.shape[1]), bf16),
-        VMEM((n_mp * rows, w_down.shape[1]), f32),
-        VMEM((n, rows, width), bf16),
-        VMEM((n, rows, width), bf16),
+        VMEM((HALVES, n_mp * part, w_gate.shape[1]), bf16),
+        VMEM((n_mp * part, w_down.shape[1]), f32),
+        VMEM((HALVES, n, part, width), bf16),
+        VMEM((HALVES, n, part, width), bf16),
         pltpu.SemaphoreType.DMA((3,)),
     ]
-    scratch += [pltpu.SemaphoreType.DMA((n,))] * 6
+    scratch += [pltpu.SemaphoreType.DMA((n,))] * (2 + 4 * HALVES)
     scratch += [pltpu.SemaphoreType.DMA((len(bounds), 10))]
-    for first, last in bounds:
+    for _, first, last in bounds:
         wide = last - first
         scratch += [
-            VMEM((2, 2, rows, wide), f32),
-            VMEM((2, 2, rows, wide), bf16),
-            VMEM((2, 2, rows, wide), bf16),
-            VMEM((2, rows, wide), bf16),
-            VMEM((2, rows, wide), bf16),
-            VMEM((n_mp, rows, wide), bf16),
+            VMEM((2, 2, part, wide), f32),
+            VMEM((2, 2, part, wide), bf16),
+            VMEM((2, 2, part, wide), bf16),
+            VMEM((2, part, wide), bf16),
+            VMEM((2, part, wide), bf16),
+            VMEM((n_mp, part, wide), bf16),
         ]
     vmem, anywhere = pl.BlockSpec(memory_space=VMEM), pl.BlockSpec(memory_space=pl.ANY)
     return pl.pallas_call(

time: 138 us -> 131 us (0.949); the launches traced: 138 us -> 129 us
  Pallas kernels: 129 us -> 120 us
    pallas_call x1, Pallas kernels: 71.8 us -> 62.7 us  [ffn(): pl.pallas_call(functools.partial(ffn_kernel, plans, bounds), out_shape=ja...]
where the time goes in v4:
time: 131 us; the launch traced here: 129 us
  Pallas kernels  120 us (92%)
  local copies, waits for them, and re-layouts  2.89 us (2%)
  matrix products  2.71 us (2%)
  other arithmetic  2.45 us (2%)
    pallas_call x1, Pallas kernels, ffn(): pl.pallas_call(functools.partial(ffn_kernel, plans, bounds), out_shape=ja...  62.7 us
    pallas_call x2, Pallas kernels, gather(): pl.pallas_call(functools.partial(gather_kernel, n), out_shape=jax.ShapeDt...  34.2 us
    pallas_call x1, Pallas kernels, exchange(): pl.pallas_call(functools.partial(exchange_kernel, plans, spread), out_sha...  8.7 us
    pallas_call x1, Pallas kernels, attention(): pl.pallas_call(attention_kernel, grid=(KV_HEADS,), out_shape=(jax.ShapeDt...  7.88 us
    pallas_call x2, Pallas kernels, simple(): pl.pallas_call(kernel, out_shape=out_shape, name=kernel.__name__)(*arrays)  6.48 us
    dot_general x1, matrix products, body(): jnp.dot(normed, w_query, preferred_element_type=jnp.float32) + query_bias  2.71 us

profile of v4, /device:TPU:5, one launch (start us, length us, event | category | flops | bytes accessed | tf_op | source)
XLA Modules:
  0.0 128.7 jit_solution(9084698477852829654)
XLA Ops:
  0.6 0.0 copy-start
  0.7 1.4 %multiply_reduce_fusion = f32[64]{0:T(128)S(1)} fusion(bf16[64,3584]{1,0:T(8,128)(2,1)} %param.11), kind=kLoop, calls=%fused_computation.3 | loop fusion | flops 688064 | bytes 459008 | tf_op jit(solution)/shard_map/reduce_sum | solution.py:564
  2.0 0.7 copy-done
  2.7 2.7 %fusion.src = bf16[64,448]{1,0:T(8,128)(2,1)} fusion(bf16[3584,448]{0,1:T(8,128)(2,1)S(1)} %copy-done, f32[3584]{0:T(1024)} %param.12, f32[64]{0:T(128)S(1)} %add_rsqrt_fusion, bf16[64,3584]{1,0:T(8,128)(2,1)} %param.11, f32[448]{0:T(512)} %param.14), kind=kOutput, calls=%fused_computation.1 | convolution fusion | flops 206495744 | bytes 3743744 | tf_op jit(solution)/shard_map/dot_general | solution.py:566
  5.4 15.3 %queries.1.q_ref = bf16[8,64,448]{2,1,0:T(8,128)(2,1)} custom-call(bf16[64,448]{1,0:T(8,128)(2,1)} %fusion.src), custom_call_target="tpu_custom_call" | custom-call | tf_op jit(solution)/shard_map/queries/pallas_call | solution.py:222
  20.7 7.9 %block_attention.1 = (bf16[8,64,448]{2,1,0:T(8,128)(2,1)}, f32[4,16,64]{2,1,0:T(8,128)}) custom-call(bf16[8,64,448]{2,1,0:T(8,128)(2,1)} %queries.1.q_ref, bf16[4,1024,128]{2,1,0:T(8,128)(2,1)} %k_ref.1, bf16[4,1024,128]{2,1,0:T(8,128)(2,1)} %v_ref.1), custom_call_target="tpu_custom_call" | custom-call | tf_op jit(solution)/shard_map/block_attention/pallas_call | solution.py:258
  28.6 8.7 %merge.1 = (bf16[8,64,448]{2,1,0:T(8,128)(2,1)}, f32[8,16,64]{2,1,0:T(8,128)}) custom-call(bf16[8,64,448]{2,1,0:T(8,128)(2,1)} %get-tuple-element.9.refs_0_, f32[4,16,64]{2,1,0:T(8,128)} %get-tuple-element.10.refs_1_), custom_call_target="tpu_custom_call" | custom-call | tf_op jit(solution)/shard_map/merge/pallas_call | solution.py:176
  37.3 2.7 %merge_kernel.1.src = bf16[64,448]{1,0:T(8,128)(2,1)} custom-call(bf16[8,64,448]{2,1,0:T(8,128)(2,1)} %get-tuple-element.11.weighted_ref, f32[8,16,64]{2,1,0:T(8,128)} %get-tuple-element.12.stat_ref), custom_call_target="tpu_custom_call" | custom-call | tf_op jit(solution)/shard_map/merge_kernel/pallas_call | solution.py:305
  40.0 18.9 %attended.1.blocks = bf16[8,64,448]{2,1,0:T(8,128)(2,1)} custom-call(bf16[64,448]{1,0:T(8,128)(2,1)} %merge_kernel.1.src), custom_call_target="tpu_custom_call" | custom-call | tf_op jit(solution)/shard_map/attended/pallas_call | solution.py:222
  58.9 1.1 convert_element_type.9
  60.0 0.8 constant_dynamic-slice_fusion.own_tokens
  60.8 3.8 %project_kernel.1 = (f32[64,448]{1,0:T(8,128)}, bf16[64,448]{1,0:T(8,128)(2,1)}, f32[1,64]{1,0:T(1,128)}) custom-call(bf16[8,64,448]{2,1,0:T(8,128)(2,1)} %attended.1.blocks, bf16[448,3584]{1,0:T(8,128)(2,1)} %bitcast.7, f32[64,448]{1,0:T(8,128)} %constant_dynamic-slice_fusion.own_tokens, f32[1,448]{1,0:T(1,128)} %bitcast.8), custom_call_target="tpu_custom_call" | custom-call | tf_op jit(solution)/shard_map/project_kernel/pallas_call | solution.py:305
  64.5 62.7 %ffn.1 = bf16[64,448]{1,0:T(8,128)(2,1)} custom-call(bf16[64,448]{1,0:T(8,128)(2,1)} %get-tuple-element.13.refs_0_, f32[1,64]{1,0:T(1,128)} %get-tuple-element.14.refs_1_, f32[64,448]{1,0:T(8,128)} %get-tuple-element.15.refs_2_, bf16[2368,896]{1,0:T(8,128)(2,1)} %bitcast.5, bf16[2368,896]{1,0:T(8,128)(2,1)} %bitcast.6, bf16[2368,896]{1,0:T(8,128)(2,1)} %refs_5_.1), custom_call_target="tpu_custom_call" | custom-call | tf_op jit(solution)/shard_map/ffn/pallas_call | solution.py:531
  127.3 1.5 %copy.14 = bf16[64,448]{1,0:T(8,128)(2,1)} copy(bf16[64,448]{1,0:T(8,128)(2,1)} %ffn.1) | data formatting | bytes 114688
  (1 shorter events, 0.0 us)
Async XLA Ops:
  0.6 2.1 %copy-start = (bf16[3584,448]{0,1:T(8,128)(2,1)S(1)}, bf16[3584,448]{0,1:T(8,128)(2,1)}, u32[]{:S(2)}) copy-start(bf16[3584,448]{0,1:T(8,128)(2,1)} %param.13) | copy-start | bytes 9633796
